TPU v7x, 256 devices: a whole 4x4x8 slice. The times are simulated.
256 devices in a mesh: pipe: 8 (over x, z_lo), tensor: 4 (over y), expert: 8 (over z_hi, core).
Axes of the slice: x: 4, y: 4, z: 8 (z_hi: 4, z_lo: 2; z = z_hi * 2 + z_lo), core: 2. Of those that a mesh axis runs over, the one named last changes fastest.
Arguments:
- tokens: bfloat16 [2, 512, 4096], P(None, 'expert'), may hold values from -6 to 6
- gains: float32 [8, 4096], P('pipe'), may hold values from 0.1 to 1.9
- route_ids: int32 [8, 2, 512, 2], P('pipe', None, 'expert'), may hold values from 0 to 7, all different within a row
- route_weights: float32 [8, 2, 512, 2], P('pipe', None, 'expert'), may hold values from 0.2 to 1
- picks: int32 [8, 2, 8, 64], P('pipe', None, 'expert'), may hold values from 0 to 63, each once within a row
- w_gate: bfloat16 [8, 8, 4096, 1536], P('pipe', 'expert', None, 'tensor'), may hold values from -0.09375 to 0.09375
- w_up: bfloat16 [8, 8, 4096, 1536], P('pipe', 'expert', None, 'tensor'), may hold values from -0.09375 to 0.09375
- w_down: bfloat16 [8, 8, 1536, 4096], P('pipe', 'expert', 'tensor'), may hold values from -0.15625 to 0.15625
Outputs:
- streams: bfloat16 [8, 2, 512, 4096], P('pipe', None, 'expert', 'tensor')
Inputs may be any that keep to these rules, and one draw needn't show every extreme that they name: `route_ids`: each token names 2 different experts; every expert is named by some token. `picks`: for every layer, micro-batch and block of 64 tokens, a permutation of 0 to 63.
All inputs are finite; a program needn't handle non-finite values.
Results may differ from a plain program's by a relative error of at most 0.025.
Values may be sent and summed in bfloat16 or wider, within the bound.
A program may use at most 64 MiB of HBM per device.

v0:
```python
import jax
import jax.numpy as jnp
from jax import lax
from jax.sharding import PartitionSpec as P

epsilon = 1e-06


def from_everyone(value, axis):
    copies = jnp.broadcast_to(value, (lax.axis_size(axis), *value.shape))
    return lax.all_to_all(copies, axis, split_axis=0, concat_axis=0, tiled=True)


def joined_along(pieces, dim):
    pieces = jnp.moveaxis(pieces, 0, dim)
    shape = pieces.shape
    return pieces.reshape(*shape[:dim], shape[dim] * shape[dim + 1], *shape[dim + 2 :])


def gather_directly(value, axis, dim):
    pieces = from_everyone(value, axis)
    return joined_along(pieces, dim)


def cut_along(value, dim, count):
    before, after = (value.shape[:dim], value.shape[dim + 1 :])
    return jnp.moveaxis(value.reshape(*before, count, -1, *after), dim, 0)


def sum_at_owner(value, axis, dim):
    pieces = cut_along(value, dim, lax.axis_size(axis))
    arrived = lax.all_to_all(pieces, axis, split_axis=0, concat_axis=0, tiled=True)
    return arrived.astype(jnp.float32).sum(axis=0)


def passed_along(block, axis, distance):
    devices = range(lax.axis_size(axis))
    route = [(i - distance, i) for i in devices if i - distance in devices]
    return lax.ppermute(block, axis, route)


def local(tokens, gains, route_ids, route_weights, picks, w_gate, w_up, w_down):
    micro_count = tokens.shape[0]
    local_tokens = tokens.shape[1]
    model_width = tokens.shape[2]
    route_count = route_ids.shape[3]
    tensor_ranks = lax.axis_size("tensor")
    groups = lax.axis_size("expert")
    sections = lax.axis_size("pipe")
    quarter = local_tokens // tensor_ranks
    capacity = 4 * quarter * route_count // (3 * groups)
    slice_width = model_width // tensor_ranks
    my_section = lax.axis_index("pipe")
    my_rank = lax.axis_index("tensor")
    gain_row = gains[0]
    gate_matrix = w_gate[0, 0]
    up_matrix = w_up[0, 0]
    down_matrix = w_down[0, 0]

    def expert_work(arrived):
        gathered = gather_directly(arrived, "tensor", 0)
        row_count = gathered.shape[0] * gathered.shape[1]
        row_block = gathered.reshape(row_count, model_width)
        gate_val = jnp.dot(row_block, gate_matrix, preferred_element_type=jnp.float32)
        up_val = jnp.dot(row_block, up_matrix, preferred_element_type=jnp.float32)
        hidden = (jax.nn.silu(gate_val) * up_val).astype(jnp.bfloat16)
        partial_sum = jnp.dot(hidden, down_matrix, preferred_element_type=jnp.float32)
        summed = sum_at_owner(partial_sum.reshape(gathered.shape).astype(jnp.bfloat16), "tensor", 0)
        return summed.astype(jnp.bfloat16)

    def expert_layer(quarter_rows, chosen, micro_index):
        section_ids = route_ids[0, micro_index][chosen]
        section_weights = route_weights[0, micro_index][chosen]
        stream_f = quarter_rows.astype(jnp.float32)
        inv_rms = lax.rsqrt(jnp.mean(stream_f * stream_f, axis=1, keepdims=True) + epsilon)
        normed = (stream_f * inv_rms * gain_row[None, :]).astype(jnp.bfloat16)
        flat_ids = section_ids.reshape(-1)
        onehot = (flat_ids[:, None] == jnp.arange(groups, dtype=jnp.int32)[None, :]).astype(
            jnp.int32
        )
        earlier = jnp.cumsum(onehot, axis=0) - onehot
        slot_index = jnp.sum(earlier * onehot, axis=1)
        kept_mask = slot_index < capacity
        target = jnp.where(kept_mask, flat_ids * capacity + slot_index, groups * capacity)
        placing = (
            jnp.arange(groups * capacity, dtype=jnp.int32)[:, None] == target[None, :]
        ).astype(jnp.bfloat16)
        routed = jnp.repeat(normed, route_count, axis=0)
        outgoing = jnp.dot(placing, routed, preferred_element_type=jnp.float32).astype(jnp.bfloat16)
        outgoing = outgoing.reshape(groups, capacity, model_width)
        returned = expert_work(
            lax.all_to_all(outgoing, "expert", split_axis=0, concat_axis=0, tiled=True)
        )
        homeward = lax.all_to_all(returned, "expert", split_axis=0, concat_axis=0, tiled=True)
        flat_back = jnp.concatenate(
            [
                homeward.reshape(groups * capacity, model_width),
                jnp.zeros((1, model_width), jnp.bfloat16),
            ],
            axis=0,
        )
        picked = flat_back[target].astype(jnp.float32).reshape(quarter, route_count, model_width)
        kept_grid = kept_mask.reshape(quarter, route_count)
        weighted = picked * (section_weights * kept_grid)[..., None]
        update = jnp.sum(weighted, axis=1)
        return (stream_f + update).astype(jnp.bfloat16)

    def run_section(stream, micro_index):
        order_all = picks[0, micro_index, 0]
        chosen = lax.dynamic_slice_in_dim(order_all, my_rank * quarter, quarter)
        permuted = stream[order_all]
        quarter_rows = lax.all_to_all(permuted, "tensor", split_axis=0, concat_axis=1, tiled=True)
        fresh_rows = expert_layer(quarter_rows, chosen, micro_index)
        spread = lax.all_to_all(fresh_rows, "tensor", split_axis=1, concat_axis=0, tiled=True)
        return jnp.zeros_like(stream).at[order_all].set(spread)

    def first_input(micro_index):
        whole = tokens[micro_index]
        return lax.dynamic_slice_in_dim(whole, my_rank * slice_width, slice_width, 1)

    def send_on(fresh):
        return passed_along(fresh, "pipe", 1)

    def section_tick(carry, tick_index):
        arrived, collected = carry
        micro_index = tick_index - my_section
        active = (micro_index >= 0) & (micro_index < micro_count)
        clipped = jnp.clip(micro_index, 0, micro_count - 1)
        stream = jnp.where(my_section == 0, first_input(clipped), arrived)
        computed = run_section(stream, clipped)
        fresh = jnp.where(active, computed, stream)
        written = collected.at[clipped].set(fresh)
        collected = jnp.where(active, written, collected)
        return ((send_on(fresh), collected), None)

    empty_state = jnp.zeros((local_tokens, slice_width), jnp.bfloat16)
    collected = jnp.zeros((micro_count, local_tokens, slice_width), jnp.bfloat16)
    ticks = jnp.arange(micro_count + sections - 1, dtype=jnp.int32)
    (final_state, collected), unused = lax.scan(section_tick, (empty_state, collected), ticks)
    return collected[None]


def solution(mesh):
    return jax.shard_map(
        local,
        mesh=mesh,
        in_specs=(
            P(None, "expert", None),
            P("pipe", None),
            P("pipe", None, "expert", None),
            P("pipe", None, "expert", None),
            P("pipe", None, "expert", None),
            P("pipe", "expert", None, "tensor"),
            P("pipe", "expert", None, "tensor"),
            P("pipe", "expert", "tensor", None),
        ),
        out_specs=P("pipe", None, "expert", "tensor"),
        check_vma=False,
    )
```

profile of v0, /device:TPU:38, one launch (start us, length us, event | category | flops | bytes accessed | tf_op | source)
XLA Modules:
  0.0 1162.5 jit_solution(10860606724604831986)
XLA Ops:
  1.3 1161.3 %while.16 = (s32[]{:T(128)}, bf16[64,1024]{1,0:T(8,128)(2,1)S(1)}, bf16[2,64,1024]{2,1,0:T(8,128)(2,1)}, s32[9]{0:T(128)}, s32[]{:T(128)}, /*index=5*/s32[1,2,1,...) while((s32[]{:T(128)}, bf16[64,1024]{1,0:T(8,128)(2,1)S(1)}, ...), condition=%wide.region_8.9_spmd, body=%wide.region_0.8_spmd.sunk | while | flops 1523243264 | bytes 51076840 | solution.py:139
  17.6 23.8 %all_to_all.92 = bf16[8,5,4096]{2,1,0:T(8,128)(2,1)S(1)} all-to-all(bf16[8,5,4096]{2,1,0:T(8,128)(2,1)S(1)} %reshape.340), channel_id=1, replica_groups=mesh['pipe'=8,'tensor'=4,'expert'=8] {'expert'}, dimensions={0} | all-to-all | bytes 655360 | tf_op jit(solution)/shard_map/while/body/eval_jaxpr/all_to_all | solution.py:92
  41.7 20.4 %all_to_all.93 = bf16[4,8,5,4096]{3,1,2,0:T(8,128)(2,1)S(1)} all-to-all(bf16[4,8,5,4096]{3,1,2,0:T(8,128)(2,1)S(1)} %broadcast_in_dim.48), channel_id=1, replica_groups=mesh['pipe'=8,'tensor'=4,'expert'=8] {'tensor'}, dimensions={0} | all-to-all | bytes 2621440 | tf_op jit(solution)/shard_map/while/body/eval_jaxpr/all_to_all | solution.py:11
  66.2 4.5 convolution_convert_fusion.5
  77.0 16.9 %all-to-all-done.3 = bf16[4,8,5,4096]{3,1,2,0:T(8,128)(2,1)S(1)} async-done(((bf16[4,8,5,4096]{3,1,2,0:T(8,128)(2,1)}), bf16[4,8,5,4096]{3,1,2,0:T(8,128)(2,1)S(1)}, u32[]{:S(2)}, u32[]{:S(2)}) %all-to-all-start.3) | async-done | bytes 1310752 | tf_op jit(solution)/shard_map/while/body/eval_jaxpr/all_to_all | solution.py:32
  99.6 17.0 %all-to-all-done.4 = bf16[8,5,4096]{2,1,0:T(8,128)(2,1)S(1)} async-done(((bf16[8,5,4096]{2,1,0:T(8,128)(2,1)}), bf16[8,5,4096]{2,1,0:T(8,128)(2,1)S(1)}, u32[]{:S(2)}, u32[]{:S(2)}) %all-to-all-start.4) | async-done | bytes 327712 | tf_op jit(solution)/shard_map/while/body/eval_jaxpr/all_to_all | solution.py:94
  123.4 5.2 all-to-all-done.5
  131.6 5.6 collective-permute-done
  152.3 20.7 %all_to_all.92 = bf16[8,5,4096]{2,1,0:T(8,128)(2,1)S(1)} all-to-all(bf16[8,5,4096]{2,1,0:T(8,128)(2,1)S(1)} %reshape.340), channel_id=1, replica_groups=mesh['pipe'=8,'tensor'=4,'expert'=8] {'expert'}, dimensions={0} | all-to-all | bytes 655360 | tf_op jit(solution)/shard_map/while/body/eval_jaxpr/all_to_all | solution.py:92
  173.4 17.2 %all_to_all.93 = bf16[4,8,5,4096]{3,1,2,0:T(8,128)(2,1)S(1)} all-to-all(bf16[4,8,5,4096]{3,1,2,0:T(8,128)(2,1)S(1)} %broadcast_in_dim.48), channel_id=1, replica_groups=mesh['pipe'=8,'tensor'=4,'expert'=8] {'tensor'}, dimensions={0} | all-to-all | bytes 2621440 | tf_op jit(solution)/shard_map/while/body/eval_jaxpr/all_to_all | solution.py:11
  205.4 13.8 %all-to-all-done.3 = bf16[4,8,5,4096]{3,1,2,0:T(8,128)(2,1)S(1)} async-done(((bf16[4,8,5,4096]{3,1,2,0:T(8,128)(2,1)}), bf16[4,8,5,4096]{3,1,2,0:T(8,128)(2,1)S(1)}, u32[]{:S(2)}, u32[]{:S(2)}) %all-to-all-start.3) | async-done | bytes 1310752 | tf_op jit(solution)/shard_map/while/body/eval_jaxpr/all_to_all | solution.py:32
  220.5 6.0 all-to-all-start.4
  227.4 17.4 %all-to-all-done.4 = bf16[8,5,4096]{2,1,0:T(8,128)(2,1)S(1)} async-done(((bf16[8,5,4096]{2,1,0:T(8,128)(2,1)}), bf16[8,5,4096]{2,1,0:T(8,128)(2,1)S(1)}, u32[]{:S(2)}, u32[]{:S(2)}) %all-to-all-start.4) | async-done | bytes 327712 | tf_op jit(solution)/shard_map/while/body/eval_jaxpr/all_to_all | solution.py:94
  251.6 5.2 all-to-all-done.5
  259.8 5.6 collective-permute-done
  280.5 20.7 %all_to_all.92 = bf16[8,5,4096]{2,1,0:T(8,128)(2,1)S(1)} all-to-all(bf16[8,5,4096]{2,1,0:T(8,128)(2,1)S(1)} %reshape.340), channel_id=1, replica_groups=mesh['pipe'=8,'tensor'=4,'expert'=8] {'expert'}, dimensions={0} | all-to-all | bytes 655360 | tf_op jit(solution)/shard_map/while/body/eval_jaxpr/all_to_all | solution.py:92
  301.6 17.1 %all_to_all.93 = bf16[4,8,5,4096]{3,1,2,0:T(8,128)(2,1)S(1)} all-to-all(bf16[4,8,5,4096]{3,1,2,0:T(8,128)(2,1)S(1)} %broadcast_in_dim.48), channel_id=1, replica_groups=mesh['pipe'=8,'tensor'=4,'expert'=8] {'tensor'}, dimensions={0} | all-to-all | bytes 2621440 | tf_op jit(solution)/shard_map/while/body/eval_jaxpr/all_to_all | solution.py:11
  333.6 13.5 %all-to-all-done.3 = bf16[4,8,5,4096]{3,1,2,0:T(8,128)(2,1)S(1)} async-done(((bf16[4,8,5,4096]{3,1,2,0:T(8,128)(2,1)}), bf16[4,8,5,4096]{3,1,2,0:T(8,128)(2,1)S(1)}, u32[]{:S(2)}, u32[]{:S(2)}) %all-to-all-start.3) | async-done | bytes 1310752 | tf_op jit(solution)/shard_map/while/body/eval_jaxpr/all_to_all | solution.py:32
  348.3 6.4 all-to-all-start.4
  355.6 17.4 %all-to-all-done.4 = bf16[8,5,4096]{2,1,0:T(8,128)(2,1)S(1)} async-done(((bf16[8,5,4096]{2,1,0:T(8,128)(2,1)}), bf16[8,5,4096]{2,1,0:T(8,128)(2,1)S(1)}, u32[]{:S(2)}, u32[]{:S(2)}) %all-to-all-start.4) | async-done | bytes 327712 | tf_op jit(solution)/shard_map/while/body/eval_jaxpr/all_to_all | solution.py:94
  379.8 5.2 all-to-all-done.5
  388.0 5.6 collective-permute-done
  408.7 20.7 %all_to_all.92 = bf16[8,5,4096]{2,1,0:T(8,128)(2,1)S(1)} all-to-all(bf16[8,5,4096]{2,1,0:T(8,128)(2,1)S(1)} %reshape.340), channel_id=1, replica_groups=mesh['pipe'=8,'tensor'=4,'expert'=8] {'expert'}, dimensions={0} | all-to-all | bytes 655360 | tf_op jit(solution)/shard_map/while/body/eval_jaxpr/all_to_all | solution.py:92
  429.8 17.1 %all_to_all.93 = bf16[4,8,5,4096]{3,1,2,0:T(8,128)(2,1)S(1)} all-to-all(bf16[4,8,5,4096]{3,1,2,0:T(8,128)(2,1)S(1)} %broadcast_in_dim.48), channel_id=1, replica_groups=mesh['pipe'=8,'tensor'=4,'expert'=8] {'tensor'}, dimensions={0} | all-to-all | bytes 2621440 | tf_op jit(solution)/shard_map/while/body/eval_jaxpr/all_to_all | solution.py:11
  461.8 13.5 %all-to-all-done.3 = bf16[4,8,5,4096]{3,1,2,0:T(8,128)(2,1)S(1)} async-done(((bf16[4,8,5,4096]{3,1,2,0:T(8,128)(2,1)}), bf16[4,8,5,4096]{3,1,2,0:T(8,128)(2,1)S(1)}, u32[]{:S(2)}, u32[]{:S(2)}) %all-to-all-start.3) | async-done | bytes 1310752 | tf_op jit(solution)/shard_map/while/body/eval_jaxpr/all_to_all | solution.py:32
  476.5 6.4 all-to-all-start.4
  483.8 17.4 %all-to-all-done.4 = bf16[8,5,4096]{2,1,0:T(8,128)(2,1)S(1)} async-done(((bf16[8,5,4096]{2,1,0:T(8,128)(2,1)}), bf16[8,5,4096]{2,1,0:T(8,128)(2,1)S(1)}, u32[]{:S(2)}, u32[]{:S(2)}) %all-to-all-start.4) | async-done | bytes 327712 | tf_op jit(solution)/shard_map/while/body/eval_jaxpr/all_to_all | solution.py:94
  508.0 5.2 all-to-all-done.5
  516.2 5.6 collective-permute-done
  536.9 20.7 %all_to_all.92 = bf16[8,5,4096]{2,1,0:T(8,128)(2,1)S(1)} all-to-all(bf16[8,5,4096]{2,1,0:T(8,128)(2,1)S(1)} %reshape.340), channel_id=1, replica_groups=mesh['pipe'=8,'tensor'=4,'expert'=8] {'expert'}, dimensions={0} | all-to-all | bytes 655360 | tf_op jit(solution)/shard_map/while/body/eval_jaxpr/all_to_all | solution.py:92
  558.0 17.1 %all_to_all.93 = bf16[4,8,5,4096]{3,1,2,0:T(8,128)(2,1)S(1)} all-to-all(bf16[4,8,5,4096]{3,1,2,0:T(8,128)(2,1)S(1)} %broadcast_in_dim.48), channel_id=1, replica_groups=mesh['pipe'=8,'tensor'=4,'expert'=8] {'tensor'}, dimensions={0} | all-to-all | bytes 2621440 | tf_op jit(solution)/shard_map/while/body/eval_jaxpr/all_to_all | solution.py:11
  589.9 13.5 %all-to-all-done.3 = bf16[4,8,5,4096]{3,1,2,0:T(8,128)(2,1)S(1)} async-done(((bf16[4,8,5,4096]{3,1,2,0:T(8,128)(2,1)}), bf16[4,8,5,4096]{3,1,2,0:T(8,128)(2,1)S(1)}, u32[]{:S(2)}, u32[]{:S(2)}) %all-to-all-start.3) | async-done | bytes 1310752 | tf_op jit(solution)/shard_map/while/body/eval_jaxpr/all_to_all | solution.py:32
  604.7 6.4 all-to-all-start.4
  612.0 17.4 %all-to-all-done.4 = bf16[8,5,4096]{2,1,0:T(8,128)(2,1)S(1)} async-done(((bf16[8,5,4096]{2,1,0:T(8,128)(2,1)}), bf16[8,5,4096]{2,1,0:T(8,128)(2,1)S(1)}, u32[]{:S(2)}, u32[]{:S(2)}) %all-to-all-start.4) | async-done | bytes 327712 | tf_op jit(solution)/shard_map/while/body/eval_jaxpr/all_to_all | solution.py:94
  636.2 5.2 all-to-all-done.5
  644.3 5.6 collective-permute-done
  665.0 20.7 %all_to_all.92 = bf16[8,5,4096]{2,1,0:T(8,128)(2,1)S(1)} all-to-all(bf16[8,5,4096]{2,1,0:T(8,128)(2,1)S(1)} %reshape.340), channel_id=1, replica_groups=mesh['pipe'=8,'tensor'=4,'expert'=8] {'expert'}, dimensions={0} | all-to-all | bytes 655360 | tf_op jit(solution)/shard_map/while/body/eval_jaxpr/all_to_all | solution.py:92
  686.2 17.1 %all_to_all.93 = bf16[4,8,5,4096]{3,1,2,0:T(8,128)(2,1)S(1)} all-to-all(bf16[4,8,5,4096]{3,1,2,0:T(8,128)(2,1)S(1)} %broadcast_in_dim.48), channel_id=1, replica_groups=mesh['pipe'=8,'tensor'=4,'expert'=8] {'tensor'}, dimensions={0} | all-to-all | bytes 2621440 | tf_op jit(solution)/shard_map/while/body/eval_jaxpr/all_to_all | solution.py:11
  718.1 13.5 %all-to-all-done.3 = bf16[4,8,5,4096]{3,1,2,0:T(8,128)(2,1)S(1)} async-done(((bf16[4,8,5,4096]{3,1,2,0:T(8,128)(2,1)}), bf16[4,8,5,4096]{3,1,2,0:T(8,128)(2,1)S(1)}, u32[]{:S(2)}, u32[]{:S(2)}) %all-to-all-start.3) | async-done | bytes 1310752 | tf_op jit(solution)/shard_map/while/body/eval_jaxpr/all_to_all | solution.py:32
  732.9 6.3 all-to-all-start.4
  740.1 17.4 %all-to-all-done.4 = bf16[8,5,4096]{2,1,0:T(8,128)(2,1)S(1)} async-done(((bf16[8,5,4096]{2,1,0:T(8,128)(2,1)}), bf16[8,5,4096]{2,1,0:T(8,128)(2,1)S(1)}, u32[]{:S(2)}, u32[]{:S(2)}) %all-to-all-start.4) | async-done | bytes 327712 | tf_op jit(solution)/shard_map/while/body/eval_jaxpr/all_to_all | solution.py:94
  764.3 5.2 all-to-all-done.5
  772.5 5.6 collective-permute-done
  793.2 20.7 %all_to_all.92 = bf16[8,5,4096]{2,1,0:T(8,128)(2,1)S(1)} all-to-all(bf16[8,5,4096]{2,1,0:T(8,128)(2,1)S(1)} %reshape.340), channel_id=1, replica_groups=mesh['pipe'=8,'tensor'=4,'expert'=8] {'expert'}, dimensions={0} | all-to-all | bytes 655360 | tf_op jit(solution)/shard_map/while/body/eval_jaxpr/all_to_all | solution.py:92
  814.3 17.1 %all_to_all.93 = bf16[4,8,5,4096]{3,1,2,0:T(8,128)(2,1)S(1)} all-to-all(bf16[4,8,5,4096]{3,1,2,0:T(8,128)(2,1)S(1)} %broadcast_in_dim.48), channel_id=1, replica_groups=mesh['pipe'=8,'tensor'=4,'expert'=8] {'tensor'}, dimensions={0} | all-to-all | bytes 2621440 | tf_op jit(solution)/shard_map/while/body/eval_jaxpr/all_to_all | solution.py:11
  846.3 13.5 %all-to-all-done.3 = bf16[4,8,5,4096]{3,1,2,0:T(8,128)(2,1)S(1)} async-done(((bf16[4,8,5,4096]{3,1,2,0:T(8,128)(2,1)}), bf16[4,8,5,4096]{3,1,2,0:T(8,128)(2,1)S(1)}, u32[]{:S(2)}, u32[]{:S(2)}) %all-to-all-start.3) | async-done | bytes 1310752 | tf_op jit(solution)/shard_map/while/body/eval_jaxpr/all_to_all | solution.py:32
  861.0 6.3 all-to-all-start.4
  868.3 17.4 %all-to-all-done.4 = bf16[8,5,4096]{2,1,0:T(8,128)(2,1)S(1)} async-done(((bf16[8,5,4096]{2,1,0:T(8,128)(2,1)}), bf16[8,5,4096]{2,1,0:T(8,128)(2,1)S(1)}, u32[]{:S(2)}, u32[]{:S(2)}) %all-to-all-start.4) | async-done | bytes 327712 | tf_op jit(solution)/shard_map/while/body/eval_jaxpr/all_to_all | solution.py:94
  892.5 5.2 all-to-all-done.5
  900.6 5.6 collective-permute-done
  921.3 20.7 %all_to_all.92 = bf16[8,5,4096]{2,1,0:T(8,128)(2,1)S(1)} all-to-all(bf16[8,5,4096]{2,1,0:T(8,128)(2,1)S(1)} %reshape.340), channel_id=1, replica_groups=mesh['pipe'=8,'tensor'=4,'expert'=8] {'expert'}, dimensions={0} | all-to-all | bytes 655360 | tf_op jit(solution)/shard_map/while/body/eval_jaxpr/all_to_all | solution.py:92
  942.4 17.1 %all_to_all.93 = bf16[4,8,5,4096]{3,1,2,0:T(8,128)(2,1)S(1)} all-to-all(bf16[4,8,5,4096]{3,1,2,0:T(8,128)(2,1)S(1)} %broadcast_in_dim.48), channel_id=1, replica_groups=mesh['pipe'=8,'tensor'=4,'expert'=8] {'tensor'}, dimensions={0} | all-to-all | bytes 2621440 | tf_op jit(solution)/shard_map/while/body/eval_jaxpr/all_to_all | solution.py:11
  974.4 13.5 %all-to-all-done.3 = bf16[4,8,5,4096]{3,1,2,0:T(8,128)(2,1)S(1)} async-done(((bf16[4,8,5,4096]{3,1,2,0:T(8,128)(2,1)}), bf16[4,8,5,4096]{3,1,2,0:T(8,128)(2,1)S(1)}, u32[]{:S(2)}, u32[]{:S(2)}) %all-to-all-start.3) | async-done | bytes 1310752 | tf_op jit(solution)/shard_map/while/body/eval_jaxpr/all_to_all | solution.py:32
  989.1 6.4 all-to-all-start.4
  996.4 17.4 %all-to-all-done.4 = bf16[8,5,4096]{2,1,0:T(8,128)(2,1)S(1)} async-done(((bf16[8,5,4096]{2,1,0:T(8,128)(2,1)}), bf16[8,5,4096]{2,1,0:T(8,128)(2,1)S(1)}, u32[]{:S(2)}, u32[]{:S(2)}) %all-to-all-start.4) | async-done | bytes 327712 | tf_op jit(solution)/shard_map/while/body/eval_jaxpr/all_to_all | solution.py:94
  1020.7 5.2 all-to-all-done.5
  1028.8 5.6 collective-permute-done
  1049.5 20.7 %all_to_all.92 = bf16[8,5,4096]{2,1,0:T(8,128)(2,1)S(1)} all-to-all(bf16[8,5,4096]{2,1,0:T(8,128)(2,1)S(1)} %reshape.340), channel_id=1, replica_groups=mesh['pipe'=8,'tensor'=4,'expert'=8] {'expert'}, dimensions={0} | all-to-all | bytes 655360 | tf_op jit(solution)/shard_map/while/body/eval_jaxpr/all_to_all | solution.py:92
  1070.6 17.1 %all_to_all.93 = bf16[4,8,5,4096]{3,1,2,0:T(8,128)(2,1)S(1)} all-to-all(bf16[4,8,5,4096]{3,1,2,0:T(8,128)(2,1)S(1)} %broadcast_in_dim.48), channel_id=1, replica_groups=mesh['pipe'=8,'tensor'=4,'expert'=8] {'tensor'}, dimensions={0} | all-to-all | bytes 2621440 | tf_op jit(solution)/shard_map/while/body/eval_jaxpr/all_to_all | solution.py:11
  1102.6 13.5 %all-to-all-done.3 = bf16[4,8,5,4096]{3,1,2,0:T(8,128)(2,1)S(1)} async-done(((bf16[4,8,5,4096]{3,1,2,0:T(8,128)(2,1)}), bf16[4,8,5,4096]{3,1,2,0:T(8,128)(2,1)S(1)}, u32[]{:S(2)}, u32[]{:S(2)}) %all-to-all-start.3) | async-done | bytes 1310752 | tf_op jit(solution)/shard_map/while/body/eval_jaxpr/all_to_all | solution.py:32
  1117.3 6.4 all-to-all-start.4
  1124.6 17.4 %all-to-all-done.4 = bf16[8,5,4096]{2,1,0:T(8,128)(2,1)S(1)} async-done(((bf16[8,5,4096]{2,1,0:T(8,128)(2,1)}), bf16[8,5,4096]{2,1,0:T(8,128)(2,1)S(1)}, u32[]{:S(2)}, u32[]{:S(2)}) %all-to-all-start.4) | async-done | bytes 327712 | tf_op jit(solution)/shard_map/while/body/eval_jaxpr/all_to_all | solution.py:94
  1148.8 5.2 all-to-all-done.5
  1157.0 5.6 collective-permute-done
  (687 shorter events, 373.8 us)
Async XLA Ops:
  1.3 15.5 %copy-start.4 = (f32[1,4096]{1,0:T(1,128)S(1)}, f32[1,4096]{1,0:T(1,128)}, u32[]{:S(2)}) copy-start(f32[1,4096]{1,0:T(1,128)} %get-tuple-element.469) | copy-start | bytes 49156 | tf_op jit(solution)/shard_map/while
  6.1 10.4 all-to-all-start
  16.6 24.8 %copy-start = (bf16[4,16,1024]{2,1,0:T(8,128)(2,1)}, bf16[4,16,1024]{2,1,0:T(8,128)(2,1)S(1)}, u32[]{:S(2)}) copy-start(bf16[4,16,1024]{2,1,0:T(8,128)(2,1)S(1)} %all-to-all-done) | copy-start | bytes 393220 | tf_op jit(solution)/shard_map/while
  73.3 20.6 %all-to-all-start.3 = ((bf16[4,8,5,4096]{3,1,2,0:T(8,128)(2,1)}), bf16[4,8,5,4096]{3,1,2,0:T(8,128)(2,1)S(1)}, u32[]{:S(2)}, u32[]{:S(2)}) async-start(bf16[4,8,5,4096]{3,1,2,0:T(8,128)(2,1)} %copy.62), calls=%async_computation.3 | async-start | bytes 2621440 | tf_op jit(solution)/shard_map/while/body/eval_jaxpr/all_to_all | solution.py:32
  77.0 21.7 %copy-start.7 = (f32[1,2,64,2]{2,3,1,0:T(2,128)S(1)}, f32[1,2,64,2]{2,3,1,0:T(2,128)}, u32[]{:S(2)}) copy-start(f32[1,2,64,2]{2,3,1,0:T(2,128)} %get-tuple-element.473) | copy-start | bytes 3076 | tf_op jit(solution)/shard_map/while
  95.2 21.5 %all-to-all-start.4 = ((bf16[8,5,4096]{2,1,0:T(8,128)(2,1)}), bf16[8,5,4096]{2,1,0:T(8,128)(2,1)S(1)}, u32[]{:S(2)}, u32[]{:S(2)}) async-start(bf16[8,5,4096]{2,1,0:T(8,128)(2,1)} %copy.63), calls=%async_computation.4 | async-start | bytes 1048576 | tf_op jit(solution)/shard_map/while/body/eval_jaxpr/all_to_all | solution.py:94
  119.3 9.3 all-to-all-start.5
  130.3 6.9 collective-permute-start
  142.0 9.3 all-to-all-start
  151.2 21.8 %copy-start = (bf16[4,16,1024]{2,1,0:T(8,128)(2,1)}, bf16[4,16,1024]{2,1,0:T(8,128)(2,1)S(1)}, u32[]{:S(2)}) copy-start(bf16[4,16,1024]{2,1,0:T(8,128)(2,1)S(1)} %all-to-all-done) | copy-start | bytes 393220 | tf_op jit(solution)/shard_map/while
  201.7 17.6 %all-to-all-start.3 = ((bf16[4,8,5,4096]{3,1,2,0:T(8,128)(2,1)}), bf16[4,8,5,4096]{3,1,2,0:T(8,128)(2,1)S(1)}, u32[]{:S(2)}, u32[]{:S(2)}) async-start(bf16[4,8,5,4096]{3,1,2,0:T(8,128)(2,1)} %copy.62), calls=%async_computation.3 | async-start | bytes 2621440 | tf_op jit(solution)/shard_map/while/body/eval_jaxpr/all_to_all | solution.py:32
  205.4 21.1 %copy-start.7 = (f32[1,2,64,2]{2,3,1,0:T(2,128)S(1)}, f32[1,2,64,2]{2,3,1,0:T(2,128)}, u32[]{:S(2)}) copy-start(f32[1,2,64,2]{2,3,1,0:T(2,128)} %get-tuple-element.473) | copy-start | bytes 3076 | tf_op jit(solution)/shard_map/while
  220.5 24.3 %all-to-all-start.4 = ((bf16[8,5,4096]{2,1,0:T(8,128)(2,1)}), bf16[8,5,4096]{2,1,0:T(8,128)(2,1)S(1)}, u32[]{:S(2)}, u32[]{:S(2)}) async-start(bf16[8,5,4096]{2,1,0:T(8,128)(2,1)} %copy.63), calls=%async_computation.4 | async-start | bytes 1048576 | tf_op jit(solution)/shard_map/while/body/eval_jaxpr/all_to_all | solution.py:94
  247.5 9.3 all-to-all-start.5
  258.5 6.9 collective-permute-start
  270.2 9.3 all-to-all-start
  279.5 21.8 %copy-start = (bf16[4,16,1024]{2,1,0:T(8,128)(2,1)}, bf16[4,16,1024]{2,1,0:T(8,128)(2,1)S(1)}, u32[]{:S(2)}) copy-start(bf16[4,16,1024]{2,1,0:T(8,128)(2,1)S(1)} %all-to-all-done) | copy-start | bytes 393220 | tf_op jit(solution)/shard_map/while
  329.9 17.2 %all-to-all-start.3 = ((bf16[4,8,5,4096]{3,1,2,0:T(8,128)(2,1)}), bf16[4,8,5,4096]{3,1,2,0:T(8,128)(2,1)S(1)}, u32[]{:S(2)}, u32[]{:S(2)}) async-start(bf16[4,8,5,4096]{3,1,2,0:T(8,128)(2,1)} %copy.62), calls=%async_computation.3 | async-start | bytes 2621440 | tf_op jit(solution)/shard_map/while/body/eval_jaxpr/all_to_all | solution.py:32
  333.5 21.2 %copy-start.7 = (f32[1,2,64,2]{2,3,1,0:T(2,128)S(1)}, f32[1,2,64,2]{2,3,1,0:T(2,128)}, u32[]{:S(2)}) copy-start(f32[1,2,64,2]{2,3,1,0:T(2,128)} %get-tuple-element.473) | copy-start | bytes 3076 | tf_op jit(solution)/shard_map/while
  348.3 24.7 %all-to-all-start.4 = ((bf16[8,5,4096]{2,1,0:T(8,128)(2,1)}), bf16[8,5,4096]{2,1,0:T(8,128)(2,1)S(1)}, u32[]{:S(2)}, u32[]{:S(2)}) async-start(bf16[8,5,4096]{2,1,0:T(8,128)(2,1)} %copy.63), calls=%async_computation.4 | async-start | bytes 1048576 | tf_op jit(solution)/shard_map/while/body/eval_jaxpr/all_to_all | solution.py:94
  375.7 9.3 all-to-all-start.5
  386.7 6.9 collective-permute-start
  398.4 9.3 all-to-all-start
  407.7 21.8 %copy-start = (bf16[4,16,1024]{2,1,0:T(8,128)(2,1)}, bf16[4,16,1024]{2,1,0:T(8,128)(2,1)S(1)}, u32[]{:S(2)}) copy-start(bf16[4,16,1024]{2,1,0:T(8,128)(2,1)S(1)} %all-to-all-done) | copy-start | bytes 393220 | tf_op jit(solution)/shard_map/while
  458.0 17.2 %all-to-all-start.3 = ((bf16[4,8,5,4096]{3,1,2,0:T(8,128)(2,1)}), bf16[4,8,5,4096]{3,1,2,0:T(8,128)(2,1)S(1)}, u32[]{:S(2)}, u32[]{:S(2)}) async-start(bf16[4,8,5,4096]{3,1,2,0:T(8,128)(2,1)} %copy.62), calls=%async_computation.3 | async-start | bytes 2621440 | tf_op jit(solution)/shard_map/while/body/eval_jaxpr/all_to_all | solution.py:32
  461.7 21.2 %copy-start.7 = (f32[1,2,64,2]{2,3,1,0:T(2,128)S(1)}, f32[1,2,64,2]{2,3,1,0:T(2,128)}, u32[]{:S(2)}) copy-start(f32[1,2,64,2]{2,3,1,0:T(2,128)} %get-tuple-element.473) | copy-start | bytes 3076 | tf_op jit(solution)/shard_map/while
  476.5 24.7 %all-to-all-start.4 = ((bf16[8,5,4096]{2,1,0:T(8,128)(2,1)}), bf16[8,5,4096]{2,1,0:T(8,128)(2,1)S(1)}, u32[]{:S(2)}, u32[]{:S(2)}) async-start(bf16[8,5,4096]{2,1,0:T(8,128)(2,1)} %copy.63), calls=%async_computation.4 | async-start | bytes 1048576 | tf_op jit(solution)/shard_map/while/body/eval_jaxpr/all_to_all | solution.py:94
  503.9 9.3 all-to-all-start.5
  514.9 6.9 collective-permute-start
  526.6 9.3 all-to-all-start
  535.8 21.8 %copy-start = (bf16[4,16,1024]{2,1,0:T(8,128)(2,1)}, bf16[4,16,1024]{2,1,0:T(8,128)(2,1)S(1)}, u32[]{:S(2)}) copy-start(bf16[4,16,1024]{2,1,0:T(8,128)(2,1)S(1)} %all-to-all-done) | copy-start | bytes 393220 | tf_op jit(solution)/shard_map/while
  586.2 17.2 %all-to-all-start.3 = ((bf16[4,8,5,4096]{3,1,2,0:T(8,128)(2,1)}), bf16[4,8,5,4096]{3,1,2,0:T(8,128)(2,1)S(1)}, u32[]{:S(2)}, u32[]{:S(2)}) async-start(bf16[4,8,5,4096]{3,1,2,0:T(8,128)(2,1)} %copy.62), calls=%async_computation.3 | async-start | bytes 2621440 | tf_op jit(solution)/shard_map/while/body/eval_jaxpr/all_to_all | solution.py:32
  589.9 21.1 %copy-start.7 = (f32[1,2,64,2]{2,3,1,0:T(2,128)S(1)}, f32[1,2,64,2]{2,3,1,0:T(2,128)}, u32[]{:S(2)}) copy-start(f32[1,2,64,2]{2,3,1,0:T(2,128)} %get-tuple-element.473) | copy-start | bytes 3076 | tf_op jit(solution)/shard_map/while
  604.7 24.7 %all-to-all-start.4 = ((bf16[8,5,4096]{2,1,0:T(8,128)(2,1)}), bf16[8,5,4096]{2,1,0:T(8,128)(2,1)S(1)}, u32[]{:S(2)}, u32[]{:S(2)}) async-start(bf16[8,5,4096]{2,1,0:T(8,128)(2,1)} %copy.63), calls=%async_computation.4 | async-start | bytes 1048576 | tf_op jit(solution)/shard_map/while/body/eval_jaxpr/all_to_all | solution.py:94
  632.1 9.3 all-to-all-start.5
  643.0 6.9 collective-permute-start
  654.7 9.3 all-to-all-start
  664.0 21.8 %copy-start = (bf16[4,16,1024]{2,1,0:T(8,128)(2,1)}, bf16[4,16,1024]{2,1,0:T(8,128)(2,1)S(1)}, u32[]{:S(2)}) copy-start(bf16[4,16,1024]{2,1,0:T(8,128)(2,1)S(1)} %all-to-all-done) | copy-start | bytes 393220 | tf_op jit(solution)/shard_map/while
  714.4 17.2 %all-to-all-start.3 = ((bf16[4,8,5,4096]{3,1,2,0:T(8,128)(2,1)}), bf16[4,8,5,4096]{3,1,2,0:T(8,128)(2,1)S(1)}, u32[]{:S(2)}, u32[]{:S(2)}) async-start(bf16[4,8,5,4096]{3,1,2,0:T(8,128)(2,1)} %copy.62), calls=%async_computation.3 | async-start | bytes 2621440 | tf_op jit(solution)/shard_map/while/body/eval_jaxpr/all_to_all | solution.py:32
  718.1 21.1 %copy-start.7 = (f32[1,2,64,2]{2,3,1,0:T(2,128)S(1)}, f32[1,2,64,2]{2,3,1,0:T(2,128)}, u32[]{:S(2)}) copy-start(f32[1,2,64,2]{2,3,1,0:T(2,128)} %get-tuple-element.473) | copy-start | bytes 3076 | tf_op jit(solution)/shard_map/while
  732.9 24.7 %all-to-all-start.4 = ((bf16[8,5,4096]{2,1,0:T(8,128)(2,1)}), bf16[8,5,4096]{2,1,0:T(8,128)(2,1)S(1)}, u32[]{:S(2)}, u32[]{:S(2)}) async-start(bf16[8,5,4096]{2,1,0:T(8,128)(2,1)} %copy.63), calls=%async_computation.4 | async-start | bytes 1048576 | tf_op jit(solution)/shard_map/while/body/eval_jaxpr/all_to_all | solution.py:94
  760.2 9.3 all-to-all-start.5
  771.2 6.9 collective-permute-start
  782.9 9.3 all-to-all-start
  792.2 21.8 %copy-start = (bf16[4,16,1024]{2,1,0:T(8,128)(2,1)}, bf16[4,16,1024]{2,1,0:T(8,128)(2,1)S(1)}, u32[]{:S(2)}) copy-start(bf16[4,16,1024]{2,1,0:T(8,128)(2,1)S(1)} %all-to-all-done) | copy-start | bytes 393220 | tf_op jit(solution)/shard_map/while
  842.6 17.2 %all-to-all-start.3 = ((bf16[4,8,5,4096]{3,1,2,0:T(8,128)(2,1)}), bf16[4,8,5,4096]{3,1,2,0:T(8,128)(2,1)S(1)}, u32[]{:S(2)}, u32[]{:S(2)}) async-start(bf16[4,8,5,4096]{3,1,2,0:T(8,128)(2,1)} %copy.62), calls=%async_computation.3 | async-start | bytes 2621440 | tf_op jit(solution)/shard_map/while/body/eval_jaxpr/all_to_all | solution.py:32
  846.2 21.1 %copy-start.7 = (f32[1,2,64,2]{2,3,1,0:T(2,128)S(1)}, f32[1,2,64,2]{2,3,1,0:T(2,128)}, u32[]{:S(2)}) copy-start(f32[1,2,64,2]{2,3,1,0:T(2,128)} %get-tuple-element.473) | copy-start | bytes 3076 | tf_op jit(solution)/shard_map/while
  861.0 24.7 %all-to-all-start.4 = ((bf16[8,5,4096]{2,1,0:T(8,128)(2,1)}), bf16[8,5,4096]{2,1,0:T(8,128)(2,1)S(1)}, u32[]{:S(2)}, u32[]{:S(2)}) async-start(bf16[8,5,4096]{2,1,0:T(8,128)(2,1)} %copy.63), calls=%async_computation.4 | async-start | bytes 1048576 | tf_op jit(solution)/shard_map/while/body/eval_jaxpr/all_to_all | solution.py:94
  888.4 9.3 all-to-all-start.5
  899.3 6.9 collective-permute-start
  911.0 9.3 all-to-all-start
  920.3 21.8 %copy-start = (bf16[4,16,1024]{2,1,0:T(8,128)(2,1)}, bf16[4,16,1024]{2,1,0:T(8,128)(2,1)S(1)}, u32[]{:S(2)}) copy-start(bf16[4,16,1024]{2,1,0:T(8,128)(2,1)S(1)} %all-to-all-done) | copy-start | bytes 393220 | tf_op jit(solution)/shard_map/while
  970.7 17.2 %all-to-all-start.3 = ((bf16[4,8,5,4096]{3,1,2,0:T(8,128)(2,1)}), bf16[4,8,5,4096]{3,1,2,0:T(8,128)(2,1)S(1)}, u32[]{:S(2)}, u32[]{:S(2)}) async-start(bf16[4,8,5,4096]{3,1,2,0:T(8,128)(2,1)} %copy.62), calls=%async_computation.3 | async-start | bytes 2621440 | tf_op jit(solution)/shard_map/while/body/eval_jaxpr/all_to_all | solution.py:32
  974.4 21.2 %copy-start.7 = (f32[1,2,64,2]{2,3,1,0:T(2,128)S(1)}, f32[1,2,64,2]{2,3,1,0:T(2,128)}, u32[]{:S(2)}) copy-start(f32[1,2,64,2]{2,3,1,0:T(2,128)} %get-tuple-element.473) | copy-start | bytes 3076 | tf_op jit(solution)/shard_map/while
  989.1 24.7 %all-to-all-start.4 = ((bf16[8,5,4096]{2,1,0:T(8,128)(2,1)}), bf16[8,5,4096]{2,1,0:T(8,128)(2,1)S(1)}, u32[]{:S(2)}, u32[]{:S(2)}) async-start(bf16[8,5,4096]{2,1,0:T(8,128)(2,1)} %copy.63), calls=%async_computation.4 | async-start | bytes 1048576 | tf_op jit(solution)/shard_map/while/body/eval_jaxpr/all_to_all | solution.py:94
  1016.5 9.3 all-to-all-start.5
  1027.5 6.9 collective-permute-start
  1039.2 9.3 all-to-all-start
  1048.5 21.8 %copy-start = (bf16[4,16,1024]{2,1,0:T(8,128)(2,1)}, bf16[4,16,1024]{2,1,0:T(8,128)(2,1)S(1)}, u32[]{:S(2)}) copy-start(bf16[4,16,1024]{2,1,0:T(8,128)(2,1)S(1)} %all-to-all-done) | copy-start | bytes 393220 | tf_op jit(solution)/shard_map/while
  1098.9 17.2 %all-to-all-start.3 = ((bf16[4,8,5,4096]{3,1,2,0:T(8,128)(2,1)}), bf16[4,8,5,4096]{3,1,2,0:T(8,128)(2,1)S(1)}, u32[]{:S(2)}, u32[]{:S(2)}) async-start(bf16[4,8,5,4096]{3,1,2,0:T(8,128)(2,1)} %copy.62), calls=%async_computation.3 | async-start | bytes 2621440 | tf_op jit(solution)/shard_map/while/body/eval_jaxpr/all_to_all | solution.py:32
  1102.6 21.1 %copy-start.7 = (f32[1,2,64,2]{2,3,1,0:T(2,128)S(1)}, f32[1,2,64,2]{2,3,1,0:T(2,128)}, u32[]{:S(2)}) copy-start(f32[1,2,64,2]{2,3,1,0:T(2,128)} %get-tuple-element.473) | copy-start | bytes 3076 | tf_op jit(solution)/shard_map/while
  1117.3 24.7 %all-to-all-start.4 = ((bf16[8,5,4096]{2,1,0:T(8,128)(2,1)}), bf16[8,5,4096]{2,1,0:T(8,128)(2,1)S(1)}, u32[]{:S(2)}, u32[]{:S(2)}) async-start(bf16[8,5,4096]{2,1,0:T(8,128)(2,1)} %copy.63), calls=%async_computation.4 | async-start | bytes 1048576 | tf_op jit(solution)/shard_map/while/body/eval_jaxpr/all_to_all | solution.py:94
  1144.7 9.3 all-to-all-start.5
  1155.7 6.9 collective-permute-start
  (62 other events, 425.6 us)
where the time goes:
time: 1180 us; the launch traced here: 1160 us
  waiting for transfers between devices  409 us (35%)
  blocking collectives  347 us (29%)
  starting transfers between devices  160 us (14%)
  local copies, waits for them, and re-layouts  115 us (10%)
  matrix products  67.1 us (6%)
  other arithmetic  56.2 us (5%)
    all_to_all x9, blocking collectives, expert_layer(): lax.all_to_all(outgoing, 'expert', split_axis=0, concat_axis=0, tiled=True)  190 us
    all_to_all x9, blocking collectives, from_everyone(): return lax.all_to_all(copies, axis, split_axis=0, concat_axis=0, tiled=True)  158 us
    all_to_all x9, waiting for transfers between devices, expert_layer(): lax.all_to_all(returned, 'expert', split_axis=0, concat_axis=0, tiled=True)  156 us
    all_to_all x9, waiting for transfers between devices, sum_at_owner(): lax.all_to_all(pieces, axis, split_axis=0, concat_axis=0, tiled=True)  125 us
    all_to_all x9, starting transfers between devices, expert_layer(): lax.all_to_all(returned, 'expert', split_axis=0, concat_axis=0, tiled=True)  54 us
    ppermute x9, waiting for transfers between devices, passed_along(): return lax.ppermute(block, axis, route)  50 us
    all_to_all x9, waiting for transfers between devices, run_section(): lax.all_to_all(fresh_rows, 'tensor', split_axis=1, concat_axis=0, tiled=T...  46.4 us
    dot_general x9, matrix products, expert_work(): jnp.dot(hidden, down_matrix, preferred_element_type=jnp.float32)  40.5 us
  transfers between devices with their start and end apart: 45, of which 45 were waited for; matrix products, arithmetic and copies ran while one was open for 3% of the time, Pallas kernels for 0%

commit v1 on v0

v1 whole, which is shorter than its diff:
```python
import jax
import jax.numpy as jnp
from jax import lax
from jax.experimental import pallas as pl
from jax.experimental.pallas import tpu as pltpu
from jax.sharding import PartitionSpec as P

EPS = 1e-06
MESH = pl.DeviceIdType.MESH
BF = jnp.bfloat16
F32 = jnp.float32
CHUNKS = 4
CAP = 5


def wait_bytes(ref, sem):
    pltpu.make_async_copy(ref, ref, sem).wait()


def relay_kernel(
    tokens, gains, rt_own, rt_next, rt_col, w_gate, w_up, w_down, out,
    wgu, wd, place, comb, hin, hnew, xs, dfirst, dout, opp, side, relay, got, rout, ret, outbuf,
    wsem, hsem, dsem, agsem, rssem, retsem, osem, fsem,
    s_tok, s_disp, s_ag, s_rs, s_ret, s_h, s_out,
):
    sec = lax.axis_index("pipe")
    rank = lax.axis_index("tensor")
    me = lax.axis_index("expert")
    last = lax.axis_size("pipe") - 1
    up1 = lax.rem(rank + 1, 4)
    dn1 = lax.rem(rank + 3, 4)
    far = lax.rem(rank + 2, 4)

    def send(src, dst, ssem, rsem, dev):
        pltpu.make_async_remote_copy(
            src_ref=src, dst_ref=dst, send_sem=ssem, recv_sem=rsem,
            device_id=dev, device_id_type=MESH,
        ).start()

    barrier = pltpu.get_barrier_semaphore()

    def greet(dev):
        pl.semaphore_signal(barrier, inc=1, device_id=dev, device_id_type=MESH)

    for o in range(1, 8):
        greet({"expert": lax.rem(me + o, 8)})
    greet({"tensor": up1})
    greet({"tensor": dn1})

    @pl.when(sec < last)
    def _():
        for e in range(8):
            greet({"pipe": sec + 1, "expert": e})

    @pl.when(sec > 0)
    def _():
        for e in range(8):
            greet({"pipe": sec - 1, "expert": e})

    def weight_copies():
        copies = []
        for q in range(4):
            copies.append((w_gate.at[pl.ds(q * 1024, 1024), :], wgu.at[q, :, pl.ds(0, 384)]))
            copies.append((w_up.at[pl.ds(q * 1024, 1024), :], wgu.at[q, :, pl.ds(384, 384)]))
        for q in range(4):
            copies.append((w_down.at[:, pl.ds(q * 1024, 1024)], wd.at[q]))
        return [pltpu.make_async_copy(a, b, wsem.at[i]) for i, (a, b) in enumerate(copies)]

    for copy in weight_copies():
        copy.start()

    slot_rows = lax.broadcasted_iota(jnp.int32, (640, 256), 0).astype(F32)
    slot_cols = lax.broadcasted_iota(jnp.int32, (256, 640), 1).astype(F32)

    def placing(rt, k):
        t = rt[k]
        hit = (slot_rows == t[0:1, :]) | (slot_rows == t[1:2, :])
        return jnp.where(hit, 1.0, 0.0).astype(BF)

    def build(k, carry):
        place[k] = placing(rt_next, k)
        c = rt_col[k]
        mix = jnp.where(slot_cols == c[:, 0:1], c[:, 2:3], 0.0)
        mix = mix + jnp.where(slot_cols == c[:, 1:2], c[:, 3:4], 0.0)
        high = mix.astype(BF)
        comb[k, 0] = high
        comb[k, 1] = (mix - high.astype(F32)).astype(BF)
        return carry

    lax.fori_loop(0, CHUNKS, build, 0)

    greeted = 9 + jnp.where(sec < last, 8, 0) + jnp.where(sec > 0, 8, 0)
    pl.semaphore_wait(barrier, greeted)

    def place_rows(matrix, rows, dest, k):
        moved = jnp.dot(matrix, rows, preferred_element_type=F32).astype(BF)
        for e in range(8):
            dest[k, e] = moved[e * 80 : (e + 1) * 80]

    my_half = me // 4

    @pl.when(sec == 0)
    def _():
        lane = pl.multiple_of(rank * 1024, 128)
        row = pl.multiple_of(lax.rem(me, 4) * 64, 64)
        for m in range(2):
            k = m * 2 + my_half
            for o in range(1, 8):
                j = lax.rem(me + o, 8)
                send(
                    tokens.at[m, :, pl.ds(pl.multiple_of(lane + j * 128, 128), 128)],
                    hin.at[k, pl.ds(row, 64), :],
                    s_tok.at[m, o - 1], hsem.at[k], {"expert": j},
                )
            pltpu.make_async_copy(
                tokens.at[m, :, pl.ds(pl.multiple_of(lane + me * 128, 128), 128)],
                hin.at[k, pl.ds(row, 64), :], hsem.at[k],
            ).start()

        def first(k, carry):
            wait_bytes(hin.at[k], hsem.at[k])
            place_rows(placing(rt_own, k), hin[k], dfirst, k)
            for o in range(1, 8):
                e = lax.rem(me + o, 8)
                send(dfirst.at[k, e], xs.at[k, 0, me], fsem.at[k], dsem.at[k, my_half], {"expert": e})
            pltpu.make_async_copy(dfirst.at[k, me], xs.at[k, 0, me], dsem.at[k, my_half]).start()
            return carry

        lax.fori_loop(0, CHUNKS, first, 0)

    for copy in weight_copies():
        copy.wait()

    lo, hi = pl.ds(0, 4), pl.ds(4, 4)
    to_up, to_dn = {"tensor": up1}, {"tensor": dn1}

    def rows_of(k, rel):
        return jnp.concatenate([xs[k, rel, j] for j in range(8)], axis=1)

    def step(k, carry):
        ssem = s_ag.at[k]
        wait_bytes(xs.at[k, 0, lo], dsem.at[k, 0])
        send(xs.at[k, 0, lo], xs.at[k, 1, lo], ssem, agsem.at[k, 0], to_up)
        wait_bytes(xs.at[k, 0, hi], dsem.at[k, 1])
        send(xs.at[k, 0, hi], xs.at[k, 2, hi], ssem, agsem.at[k, 1], to_dn)
        send(xs.at[k, 0, lo], xs.at[k, 2, lo], ssem, agsem.at[k, 2], to_dn)
        send(xs.at[k, 0, hi], xs.at[k, 1, hi], ssem, agsem.at[k, 3], to_up)

        def part(rel, origin):
            x = rows_of(k, rel).astype(F32)
            squares = jnp.sum(x * x, axis=1, keepdims=True)
            scaled = (x * gains[pl.ds(origin, 1), :]).astype(BF)
            return squares, jnp.dot(scaled, wgu[origin], preferred_element_type=F32)

        squares, both = part(0, rank)
        wait_bytes(xs.at[k, 1, lo], agsem.at[k, 0])
        send(xs.at[k, 1, lo], xs.at[k, 3, lo], ssem, agsem.at[k, 4], to_up)
        wait_bytes(xs.at[k, 2, hi], agsem.at[k, 1])
        send(xs.at[k, 2, hi], xs.at[k, 3, hi], ssem, agsem.at[k, 5], to_dn)
        wait_bytes(xs.at[k, 1, hi], agsem.at[k, 3])
        sq, b = part(1, dn1)
        squares, both = squares + sq, both + b
        wait_bytes(xs.at[k, 2, lo], agsem.at[k, 2])
        sq, b = part(2, up1)
        squares, both = squares + sq, both + b
        wait_bytes(xs.at[k, 3, lo], agsem.at[k, 4])
        wait_bytes(xs.at[k, 3, hi], agsem.at[k, 5])
        sq, b = part(3, far)
        squares, both = squares + sq, both + b
        both = both * lax.rsqrt(squares * (1.0 / 4096.0) + EPS)
        gate, up = both[:, :384], both[:, 384:]
        hidden = (gate / (1.0 + jnp.exp(-gate)) * up).astype(BF)

        def down(q):
            return jnp.dot(hidden, wd[q], preferred_element_type=F32)

        def lanes(value, j):
            return value[:, j * 128 : (j + 1) * 128]

        ssem = s_rs.at[k]
        value = down(far)
        for j in range(8):
            opp[k, j] = lanes(value, j).astype(BF)
        send(opp.at[k, lo], relay.at[k, 0], ssem, rssem.at[k, 0], to_up)
        send(opp.at[k, hi], relay.at[k, 1], ssem, rssem.at[k, 1], to_dn)
        above = down(up1)
        for j in range(4, 8):
            side[k, 0, j] = lanes(above, j).astype(BF)
        send(side.at[k, 0, hi], got.at[k, 0, hi], ssem, rssem.at[k, 2], to_up)
        below = down(dn1)
        for j in range(4):
            side[k, 1, j] = lanes(below, j).astype(BF)
        send(side.at[k, 1, lo], got.at[k, 1, lo], ssem, rssem.at[k, 3], to_dn)
        wait_bytes(relay.at[k, 0], rssem.at[k, 0])
        for j in range(4):
            side[k, 0, j] = (lanes(above, j) + relay[k, 0, j].astype(F32)).astype(BF)
        send(side.at[k, 0, lo], got.at[k, 0, lo], ssem, rssem.at[k, 4], to_up)
        wait_bytes(relay.at[k, 1], rssem.at[k, 1])
        for j in range(4, 8):
            side[k, 1, j] = (lanes(below, j) + relay[k, 1, j - 4].astype(F32)).astype(BF)
        send(side.at[k, 1, hi], got.at[k, 1, hi], ssem, rssem.at[k, 5], to_dn)
        own = down(rank)

        def give_back(j):
            total = lanes(own, j) + got[k, 0, j].astype(F32) + got[k, 1, j].astype(F32)
            rout[k, j] = total.astype(BF)

        def ship(j):
            @pl.when(me == j)
            def _():
                pltpu.make_async_copy(rout.at[k, j], ret.at[k, me], retsem.at[k]).start()

            @pl.when(me != j)
            def _():
                send(rout.at[k, j], ret.at[k, me], s_ret.at[k], retsem.at[k], {"expert": j})

        wait_bytes(got.at[k, 1, lo], rssem.at[k, 3])
        wait_bytes(got.at[k, 0, lo], rssem.at[k, 4])
        for j in range(4):
            give_back(j)
        for j in range(4):
            ship(j)
        wait_bytes(got.at[k, 0, hi], rssem.at[k, 2])
        wait_bytes(got.at[k, 1, hi], rssem.at[k, 5])
        for j in range(4, 8):
            give_back(j)
        for j in range(4, 8):
            ship(j)

        @pl.when(sec > 0)
        def _():
            wait_bytes(hin.at[k], hsem.at[k])

        wait_bytes(ret.at[k], retsem.at[k])
        back = ret[k].reshape(640, 128)
        update = jnp.dot(comb[k, 0], back, preferred_element_type=F32)
        update = update + jnp.dot(comb[k, 1], back, preferred_element_type=F32)
        fresh = (hin[k].astype(F32) + update).astype(BF)
        hnew[k] = fresh

        @pl.when(sec < last)
        def _():
            place_rows(place[k], fresh, dout, k)
            for e in range(8):
                send(
                    dout.at[k, e], xs.at[k, 0, me], s_disp.at[k], dsem.at[k, my_half],
                    {"pipe": sec + 1, "expert": e},
                )
            send(hnew.at[k], hin.at[k], s_h.at[k], hsem.at[k], {"pipe": sec + 1})

        m, half = k // 2, lax.rem(k, 2)
        mine = pl.ds(pl.multiple_of(me * 128, 128), 128)
        for i in range(4):
            owner = half * 4 + i
            block = hnew.at[k, pl.ds(i * 64, 64), :]
            place_at = outbuf.at[m, :, mine]

            @pl.when(owner == me)
            def _():
                pltpu.make_async_copy(block, place_at, osem).start()

            @pl.when(owner != me)
            def _():
                send(block, place_at, s_out.at[k, i], osem, {"expert": owner})

        return carry

    lax.fori_loop(0, CHUNKS, step, 0)

    @pl.when(sec == 0)
    def _():
        for m in range(2):
            for o in range(7):
                wait_bytes(hin.at[m, pl.ds(0, 64), :], s_tok.at[m, o])
        for k in range(CHUNKS):
            wait_bytes(dfirst.at[k, pl.ds(0, 7)], fsem.at[k])

    def drain(k, carry):
        wait_bytes(xs.at[k, pl.ds(0, 3)], s_ag.at[k])
        wait_bytes(xs.at[k, pl.ds(0, 3)], s_rs.at[k])
        wait_bytes(ret.at[k, pl.ds(0, 7)], s_ret.at[k])

        @pl.when(sec < last)
        def _():
            wait_bytes(dout.at[k], s_disp.at[k])
            wait_bytes(hnew.at[k], s_h.at[k])

        for i in range(4):
            owner = lax.rem(k, 2) * 4 + i

            @pl.when(owner != me)
            def _():
                wait_bytes(hnew.at[k, pl.ds(i * 64, 64), :], s_out.at[k, i])

        return carry

    lax.fori_loop(0, CHUNKS, drain, 0)
    wait_bytes(outbuf, osem)
    final = pltpu.make_async_copy(outbuf, out, wsem.at[0])
    final.start()
    final.wait()


def routing(route_ids, route_weights, picks):
    micro, tokens, routes = route_ids.shape
    group = lax.axis_index("expert")
    spot = jnp.arange(tokens, dtype=jnp.int32)
    place = jnp.sum(
        jnp.where(picks[:, :, None] == spot[None, None, :], spot[None, :, None], 0), axis=1
    )
    order = (place[:, :, None] * routes + jnp.arange(routes, dtype=jnp.int32)).reshape(micro, -1)
    quarter = order // (16 * routes)
    ids = route_ids.reshape(micro, -1)
    same = (ids[:, :, None] == ids[:, None, :]) & (quarter[:, :, None] == quarter[:, None, :])
    earlier = same & (order[:, None, :] < order[:, :, None])
    slot = jnp.sum(earlier.astype(jnp.int32), axis=2)
    row = ids * 80 + lax.rem(group, 4) * 20 + quarter * CAP + slot
    row = jnp.where(slot < CAP, row, -1).astype(F32).reshape(micro, tokens, routes)
    return jnp.concatenate(
        [jnp.swapaxes(row, 1, 2), jnp.swapaxes(route_weights, 1, 2)], axis=1
    )


def local(tokens, gains, route_ids, route_weights, picks, w_gate, w_up, w_down):
    mine = routing(route_ids[0], route_weights[0], picks[0, :, 0])
    sections = lax.axis_size("pipe")
    after = lax.ppermute(mine, "pipe", [(i + 1, i) for i in range(sections - 1)])
    every = lax.all_gather(jnp.stack([mine, after]), "expert")
    table = every.reshape(2, 4, 2, 2, 4, 64).transpose(2, 3, 0, 4, 1, 5).reshape(2, 4, 4, 256)
    columns = jnp.swapaxes(table[0], 1, 2)
    vmem = pl.BlockSpec(memory_space=pltpu.VMEM)
    anywhere = pl.BlockSpec(memory_space=pl.ANY)
    dma = pltpu.SemaphoreType.DMA
    out = pl.pallas_call(
        relay_kernel,
        name="relay",
        out_shape=jax.ShapeDtypeStruct((2, 64, 1024), BF),
        in_specs=[anywhere, vmem, vmem, vmem, vmem, anywhere, anywhere, anywhere],
        out_specs=anywhere,
        scratch_shapes=[
            pltpu.VMEM((4, 1024, 768), BF),
            pltpu.VMEM((4, 384, 1024), BF),
            pltpu.VMEM((CHUNKS, 640, 256), BF),
            pltpu.VMEM((CHUNKS, 2, 256, 640), BF),
            pltpu.VMEM((CHUNKS, 256, 128), BF),
            pltpu.VMEM((CHUNKS, 256, 128), BF),
            pltpu.VMEM((CHUNKS, 4, 8, 80, 128), BF),
            pltpu.VMEM((CHUNKS, 8, 80, 128), BF),
            pltpu.VMEM((CHUNKS, 8, 80, 128), BF),
            pltpu.VMEM((CHUNKS, 8, 80, 128), BF),
            pltpu.VMEM((CHUNKS, 2, 8, 80, 128), BF),
            pltpu.VMEM((CHUNKS, 2, 4, 80, 128), BF),
            pltpu.VMEM((CHUNKS, 2, 8, 80, 128), BF),
            pltpu.VMEM((CHUNKS, 8, 80, 128), BF),
            pltpu.VMEM((CHUNKS, 8, 80, 128), BF),
            pltpu.VMEM((2, 64, 1024), BF),
            dma((12,)),
            dma((CHUNKS,)),
            dma((CHUNKS, 2)),
            dma((CHUNKS, 6)),
            dma((CHUNKS, 6)),
            dma((CHUNKS,)),
            dma(()),
            dma((CHUNKS,)),
            dma((2, 7)),
            dma((CHUNKS,)),
            dma((CHUNKS,)),
            dma((CHUNKS,)),
            dma((CHUNKS,)),
            dma((CHUNKS,)),
            dma((CHUNKS, 4)),
        ],
        compiler_params=pltpu.CompilerParams(
            collective_id=0, has_side_effects=True, vmem_limit_bytes=56 * 1024 * 1024
        ),
    )(
        tokens, gains.reshape(4, 1024), table[0], table[1], columns,
        w_gate[0, 0], w_up[0, 0], w_down[0, 0],
    )
    return out[None]


def solution(mesh):
    return jax.shard_map(
        local,
        mesh=mesh,
        in_specs=(
            P(None, "expert", None),
            P("pipe", None),
            P("pipe", None, "expert", None),
            P("pipe", None, "expert", None),
            P("pipe", None, "expert", None),
            P("pipe", "expert", None, "tensor"),
            P("pipe", "expert", None, "tensor"),
            P("pipe", "expert", "tensor", None),
        ),
        out_specs=P("pipe", None, "expert", "tensor"),
        check_vma=False,
    )
```

time: 1180 us -> 356 us (0.30); the launches traced: 1160 us -> 355 us
  waiting for transfers between devices: 409 us -> 0.01 us
  blocking collectives: 347 us -> 18.2 us
  Pallas kernels: 0 us -> 324 us
  starting transfers between devices: 160 us -> 2 us
  local copies, waits for them, and re-layouts: 115 us -> 6.39 us
  matrix products: 67.1 us -> 0 us
  other arithmetic: 56.2 us -> 3.84 us
    all_to_all x36 -> x0, waiting for transfers between devices: 359 us -> none  [the longest x9 156 us: expert_layer(): lax.all_to_all(returned, 'expert', split_axis=0, concat_axis=0, tiled=True)]
    all_to_all x18 -> x0, blocking collectives: 347 us -> none  [the longest x9 190 us: expert_layer(): lax.all_to_all(outgoing, 'expert', split_axis=0, concat_axis=0, tiled=True)]
    pallas_call x0 -> x1, Pallas kernels: none -> 324 us  [local(): pl.pallas_call(relay_kernel, name='relay', out_shape=jax.ShapeDtypeStruct...]
    all_to_all x36 -> x0, starting transfers between devices: 148 us -> none  [the longest x9 54 us: expert_layer(): lax.all_to_all(returned, 'expert', split_axis=0, concat_axis=0, tiled=True)]
    dot_general x27 -> x0, matrix products: 67.1 us -> none  [the longest x9 40.5 us: expert_work(): jnp.dot(hidden, down_matrix, preferred_element_type=jnp.float32)]
    ppermute x9 -> x1, waiting for transfers between devices: 50 us -> 0.01 us  [local(): lax.ppermute(mine, 'pipe', [(i + 1, i) for i in range(sections - 1)])]
    gather x36 -> x0, local copies, waits for them, and re-layouts: 28.7 us -> none  [the longest x9 12.2 us: run_section(): permuted = stream[order_all]]
    select_n x54 -> x1, other arithmetic: 28.5 us -> 0.01 us  [routing(): quarter = order // (16 * routes)]
  transfers between devices with their start and end apart: 45 -> 1, of which waited for: 45 -> 0; matrix products, arithmetic and copies ran while one was open for 3% -> 1% of each run, Pallas kernels for 0% -> 0%
where the time goes in v1:
time: 356 us; the launch traced here: 355 us
  Pallas kernels  324 us (91%)
  blocking collectives  18.2 us (5%)
  local copies, waits for them, and re-layouts  6.39 us (2%)
  other arithmetic  3.84 us (1%)
    pallas_call x1, Pallas kernels, local(): pl.pallas_call(relay_kernel, name='relay', out_shape=jax.ShapeDtypeStruct...  324 us
    all_gather x1, blocking collectives, local(): every = lax.all_gather(jnp.stack([mine, after]), 'expert')  18.2 us
  transfers between devices with their start and end apart: 1, of which 0 were waited for; matrix products, arithmetic and copies ran while one was open for 1% of the time, Pallas kernels for 0%

profile of v1, /device:TPU:38, one launch (start us, length us, event | category | flops | bytes accessed | tf_op | source)
XLA Modules:
  0.0 354.8 jit_solution(7943863131332851853)
XLA Ops:
  0.0 0.8 select_reduce_fusion
  0.8 0.1 add.67.clone
  0.9 0.2 add.68
  1.0 0.1 add.70
  1.2 0.8 copy.33
  2.0 0.1 eq.43
  2.1 0.2 convert_reduce_fusion
  2.4 0.1 reduce_sum.22
  2.5 0.1 copy.35
  2.6 0.7 fusion.1
  3.3 0.7 fusion.3
  4.0 2.0 collective-permute-start
  6.0 0.5 broadcast.123
  6.5 1.4 reduce.3
  7.9 0.6 reshape.123.gains
  8.5 0.0 collective-permute-done
  8.5 18.2 %all-gather = f32[16,2,4,64]{3,2,1,0:T(4,128)S(1)} all-gather(f32[2,2,4,64]{3,2,1,0:T(4,128)S(1)} %pad_maximum_fusion), channel_id=2, replica_groups=mesh['pipe'=8,'tensor'=4,'expert'=8] {'expert'}, dimensions={0}, use_global_device_ids=true | all-gather | bytes 36864 | tf_op jit(solution)/shard_map/all_gather | solution.py:328
  26.7 0.4 copy.37
  27.1 0.1 fusion.4
  27.2 0.0 copy-start
  27.2 0.8 copy.39.rt_own
  28.0 0.8 copy.40.rt_next
  28.8 0.0 copy-done
  28.8 324.3 %relay.1 = bf16[2,64,1024]{2,1,0:T(8,128)(2,1)} custom-call(bf16[2,64,4096]{2,1,0:T(8,128)(2,1)} %tokens.1, f32[4,1024]{1,0:T(4,128)} %reshape.123.gains, f32[4,4,256]{2,1,0:T(4,128)} %copy.39.rt_own, f32[4,4,256]{2,1,0:T(4,128)} %copy.40.rt_next, f32[4,256,4]{2,1,0:T(8,128)} %bitcast.28, bf16[4096,384]{1,0:T(8,128)(2,1)} %bitcast.30, ...), custom_call_target="tpu_custom_call" | custom-call | tf_op jit(solution)/shard_map/relay/pallas_call | solution.py:334
  353.2 1.7 copy.43
  (4 shorter events, 0.0 us)
Async XLA Ops:
  4.0 4.5 %collective-permute-start = (f32[2,4,64]{2,1,0:T(4,128)S(1)}, f32[2,4,64]{2,1,0:T(4,128)S(1)}, u32[]{:S(2)}, u32[]{:S(2)}) collective-permute-start(f32[2,4,64]{2,1,0:T(4,128)S(1)} %get-tuple-element.10), channel_id=1, source_target_pairs={{32,0},{64,32},{96,64},{128,96},{160,128},{192,160},{224,192},{33,... | collective-permute-start | bytes 6152 | tf_op jit(solution)/shard_map/ppermute | solution.py:327
  27.2 1.6 copy-start

commit v2 on v1

v2 whole, which is shorter than its diff:
```python
import jax
import jax.numpy as jnp
from jax import lax
from jax.experimental import pallas as pl
from jax.experimental.pallas import tpu as pltpu
from jax.sharding import PartitionSpec as P

EPS = 1e-06
MESH = pl.DeviceIdType.MESH
BF = jnp.bfloat16
F32 = jnp.float32
CHUNKS = 4
CAP = 5


def wait_bytes(ref, sem):
    pltpu.make_async_copy(ref, ref, sem).wait()


def relay_kernel(
    tokens, gains, ids, route_w, picks, w_gate, w_up, w_down, out,
    wgu, wd, table, tables, place, comb, hin, hnew, xs, dfirst, dout, acc, squares, hid,
    opp, side, relay, got, rout, ret, outbuf,
    wsem, tsem, hsem, dsem, agsem, rssem, retsem, osem,
    s_tab, s_tok, s_first, s_disp, s_ag, s_rs, s_ret, s_h, s_out,
):
    sec = lax.axis_index("pipe")
    rank = lax.axis_index("tensor")
    me = lax.axis_index("expert")
    last = lax.axis_size("pipe") - 1
    up1 = lax.rem(rank + 1, 4)
    dn1 = lax.rem(rank + 3, 4)
    far = lax.rem(rank + 2, 4)
    my_half = me // 4

    def send(src, dst, ssem, rsem, dev):
        pltpu.make_async_remote_copy(
            src_ref=src, dst_ref=dst, send_sem=ssem, recv_sem=rsem,
            device_id=dev, device_id_type=MESH,
        ).start()

    barrier = pltpu.get_barrier_semaphore()

    def greet(dev):
        pl.semaphore_signal(barrier, inc=1, device_id=dev, device_id_type=MESH)

    for o in range(1, 8):
        greet({"expert": lax.rem(me + o, 8)})
    greet({"tensor": up1})
    greet({"tensor": dn1})

    @pl.when(sec < last)
    def _():
        for e in range(8):
            greet({"pipe": sec + 1, "expert": e})

    @pl.when(sec > 0)
    def _():
        for e in range(8):
            greet({"pipe": sec - 1, "expert": e})

    def weight_copies():
        copies = []
        for q in range(4):
            copies.append((w_gate.at[pl.ds(q * 1024, 1024), :], wgu.at[q, :, pl.ds(0, 384)]))
            copies.append((w_up.at[pl.ds(q * 1024, 1024), :], wgu.at[q, :, pl.ds(384, 384)]))
        for q in range(4):
            copies.append((w_down.at[:, pl.ds(q * 1024, 1024)], wd.at[q]))
        return [pltpu.make_async_copy(a, b, wsem.at[i]) for i, (a, b) in enumerate(copies)]

    for copy in weight_copies():
        copy.start()

    def iota(shape, dim):
        return lax.broadcasted_iota(jnp.int32, shape, dim).astype(F32)

    def column(row, eye):
        return jnp.sum(jnp.where(eye, row, 0.0), axis=1, keepdims=True)

    sub, lane = iota((64, 64), 0), iota((64, 64), 1)
    eye = sub == lane
    shift = (lax.rem(me, 4) * 64).astype(F32)
    spread = (iota((64, 256), 0) + shift) == iota((64, 256), 1)
    row_of = iota((8, 256), 0)
    whole = jnp.zeros((8, 256), F32)
    for m in range(2):
        picked = column(picks[m : m + 1, :].astype(F32), eye)
        spot = jnp.sum(jnp.where(picked == lane, sub, 0.0), axis=0, keepdims=True)
        spot_col = column(spot, eye)
        quarter, quarter_col = jnp.floor(spot / 16.0), jnp.floor(spot_col / 16.0)
        names = [ids[m, t : t + 1, :].astype(F32) for t in range(2)]
        name_cols = [column(n, eye) for n in names]
        for t in range(2):
            slot = jnp.zeros((1, 64), F32)
            for u in range(2):
                hit = (name_cols[u] == names[t]) & (quarter_col == quarter)
                hit = hit & (spot_col * 2.0 + u < spot * 2.0 + t)
                slot = slot + jnp.sum(jnp.where(hit, 1.0, 0.0), axis=0, keepdims=True)
            at = names[t] * 80.0 + lax.rem(me, 4).astype(F32) * 20.0 + quarter * CAP + slot
            at = jnp.where(slot < CAP, at, -1.0)
            for field, value in ((t, at), (2 + t, route_w[m, t : t + 1, :])):
                placed = jnp.where(spread, column(value, eye), 0.0)
                placed = jnp.sum(placed, axis=0, keepdims=True)
                whole = whole + jnp.where(row_of == m * 4 + field, placed, 0.0)
    table[...] = whole

    greeted = 9 + jnp.where(sec < last, 8, 0) + jnp.where(sec > 0, 8, 0)
    pl.semaphore_wait(barrier, greeted)

    @pl.when(sec == 0)
    def _():
        start = pl.multiple_of(rank * 1024, 128)
        row = pl.multiple_of(lax.rem(me, 4) * 64, 64)
        for m in range(2):
            k = m * 2 + my_half
            for o in range(1, 8):
                j = lax.rem(me + o, 8)
                send(
                    tokens.at[m, :, pl.ds(pl.multiple_of(start + j * 128, 128), 128)],
                    hin.at[k, pl.ds(row, 64), :],
                    s_tok.at[m, o - 1], hsem.at[k], {"expert": j},
                )
            pltpu.make_async_copy(
                tokens.at[m, :, pl.ds(pl.multiple_of(start + me * 128, 128), 128)],
                hin.at[k, pl.ds(row, 64), :], hsem.at[k],
            ).start()

    for o in range(1, 8):
        send(table, tables.at[0, me], s_tab.at[o - 1], tsem.at[0], {"expert": lax.rem(me + o, 8)})
    pltpu.make_async_copy(table, tables.at[0, me], tsem.at[0]).start()

    @pl.when(sec > 0)
    def _():
        for e in range(8):
            send(table, tables.at[1, me], s_tab.at[7 + e], tsem.at[1], {"pipe": sec - 1, "expert": e})

    slot_rows = iota((640, 256), 0)
    slot_cols = iota((256, 640), 1)
    eye256 = iota((256, 256), 0) == iota((256, 256), 1)

    def fields(which, k, names):
        m, half = k // 2, lax.rem(k, 2)
        rows = []
        for f in names:
            at = pl.ds(m * 4 + f, 1)
            row = tables[which, half * 4, at, :]
            for i in range(1, 4):
                row = row + tables[which, half * 4 + i, at, :]
            rows.append(row)
        return rows

    def placing(which, k):
        a, b = fields(which, k, (0, 1))
        return jnp.where((slot_rows == a) | (slot_rows == b), 1.0, 0.0).astype(BF)

    def place_rows(matrix, rows, dest, k):
        moved = jnp.dot(matrix, rows, preferred_element_type=F32).astype(BF)
        for e in range(8):
            dest[k, e] = moved[e * 80 : (e + 1) * 80]

    wait_bytes(tables.at[0], tsem.at[0])

    @pl.when(sec == 0)
    def _():
        def first(k, carry):
            matrix = placing(0, k)
            wait_bytes(hin.at[k], hsem.at[k])
            place_rows(matrix, hin[k], dfirst, k)
            for o in range(1, 8):
                e = lax.rem(me + o, 8)
                send(dfirst.at[k, e], xs.at[k, 0, me], s_first.at[k], dsem.at[k, my_half], {"expert": e})
            pltpu.make_async_copy(dfirst.at[k, me], xs.at[k, 0, me], dsem.at[k, my_half]).start()
            return carry

        lax.fori_loop(0, CHUNKS, first, 0)

    def build(k, carry):
        cols = [column(row, eye256) for row in fields(0, k, (0, 1, 2, 3))]
        mix = jnp.where(slot_cols == cols[0], cols[2], 0.0)
        mix = mix + jnp.where(slot_cols == cols[1], cols[3], 0.0)
        high = mix.astype(BF)
        comb[k, 0] = high
        comb[k, 1] = (mix - high.astype(F32)).astype(BF)
        return carry

    lax.fori_loop(0, CHUNKS, build, 0)

    @pl.when(sec < last)
    def _():
        wait_bytes(tables.at[1], tsem.at[1])

        def build_next(k, carry):
            place[k] = placing(1, k)
            return carry

        lax.fori_loop(0, CHUNKS, build_next, 0)

    for copy in weight_copies():
        copy.wait()

    lo, hi = pl.ds(0, 4), pl.ds(4, 4)
    to_up, to_dn = {"tensor": up1}, {"tensor": dn1}

    def lanes(value, j):
        return value[:, j * 128 : (j + 1) * 128]

    def part(k, rel, origin):
        x = jnp.concatenate([xs[k, rel, j] for j in range(8)], axis=1).astype(F32)
        scaled = x * gains[:, pl.ds(pl.multiple_of(origin * 1024, 128), 1024)]
        both = jnp.dot(scaled.astype(BF), wgu[origin], preferred_element_type=F32)
        return jnp.sum(x * x, axis=1, keepdims=True), both

    def gather_start(k):
        ssem = s_ag.at[k]
        wait_bytes(xs.at[k, 0, lo], dsem.at[k, 0])
        send(xs.at[k, 0, lo], xs.at[k, 1, lo], ssem, agsem.at[k, 0], to_up)
        wait_bytes(xs.at[k, 0, hi], dsem.at[k, 1])
        send(xs.at[k, 0, hi], xs.at[k, 2, hi], ssem, agsem.at[k, 1], to_dn)
        send(xs.at[k, 0, lo], xs.at[k, 2, lo], ssem, agsem.at[k, 2], to_dn)
        send(xs.at[k, 0, hi], xs.at[k, 1, hi], ssem, agsem.at[k, 3], to_up)

    def gather_relay(k):
        ssem = s_ag.at[k]
        sq, both = part(k, 0, rank)
        acc[...] = both
        squares[...] = jnp.broadcast_to(sq, (80, 128))
        wait_bytes(xs.at[k, 1, lo], agsem.at[k, 0])
        send(xs.at[k, 1, lo], xs.at[k, 3, lo], ssem, agsem.at[k, 4], to_up)
        wait_bytes(xs.at[k, 2, hi], agsem.at[k, 1])
        send(xs.at[k, 2, hi], xs.at[k, 3, hi], ssem, agsem.at[k, 5], to_dn)

    def feed_forward(k):
        both, sq = acc[...], squares[:, 0:1]
        wait_bytes(xs.at[k, 1, hi], agsem.at[k, 3])
        s, b = part(k, 1, dn1)
        sq, both = sq + s, both + b
        wait_bytes(xs.at[k, 2, lo], agsem.at[k, 2])
        s, b = part(k, 2, up1)
        sq, both = sq + s, both + b
        wait_bytes(xs.at[k, 3, lo], agsem.at[k, 4])
        wait_bytes(xs.at[k, 3, hi], agsem.at[k, 5])
        s, b = part(k, 3, far)
        sq, both = sq + s, both + b
        both = both * lax.rsqrt(sq * (1.0 / 4096.0) + EPS)
        gate, up = both[:, :384], both[:, 384:]
        hid[...] = (gate / (1.0 + jnp.exp(-gate)) * up).astype(BF)

    def down(q):
        return jnp.dot(hid[...], wd[q], preferred_element_type=F32).astype(BF)

    def sum_start(k):
        ssem = s_rs.at[k]
        value = down(far)
        for j in range(8):
            opp[k, j] = lanes(value, j)
        send(opp.at[k, lo], relay.at[k, 0], ssem, rssem.at[k, 0], to_up)
        send(opp.at[k, hi], relay.at[k, 1], ssem, rssem.at[k, 1], to_dn)
        value = down(up1)
        for j in range(8):
            side[k, 0, j] = lanes(value, j)
        send(side.at[k, 0, hi], got.at[k, 0, hi], ssem, rssem.at[k, 2], to_up)
        value = down(dn1)
        for j in range(8):
            side[k, 1, j] = lanes(value, j)
        send(side.at[k, 1, lo], got.at[k, 1, lo], ssem, rssem.at[k, 3], to_dn)
        value = down(rank)
        for j in range(8):
            rout[k, j] = lanes(value, j)

    def sum_relay(k):
        ssem = s_rs.at[k]
        wait_bytes(relay.at[k, 0], rssem.at[k, 0])
        for j in range(4):
            side[k, 0, j] = (side[k, 0, j].astype(F32) + relay[k, 0, j].astype(F32)).astype(BF)
        send(side.at[k, 0, lo], got.at[k, 0, lo], ssem, rssem.at[k, 4], to_up)
        wait_bytes(relay.at[k, 1], rssem.at[k, 1])
        for j in range(4, 8):
            side[k, 1, j] = (side[k, 1, j].astype(F32) + relay[k, 1, j - 4].astype(F32)).astype(BF)
        send(side.at[k, 1, hi], got.at[k, 1, hi], ssem, rssem.at[k, 5], to_dn)

    def give_back(k, j):
        total = rout[k, j].astype(F32) + got[k, 0, j].astype(F32) + got[k, 1, j].astype(F32)
        rout[k, j] = total.astype(BF)

    def ship(k, j):
        @pl.when(me == j)
        def _():
            pltpu.make_async_copy(rout.at[k, j], ret.at[k, me], retsem.at[k]).start()

        @pl.when(me != j)
        def _():
            send(rout.at[k, j], ret.at[k, me], s_ret.at[k], retsem.at[k], {"expert": j})

    def sum_end(k):
        wait_bytes(got.at[k, 1, lo], rssem.at[k, 3])
        wait_bytes(got.at[k, 0, lo], rssem.at[k, 4])
        for j in range(4):
            give_back(k, j)
        for j in range(4):
            ship(k, j)
        wait_bytes(got.at[k, 0, hi], rssem.at[k, 2])
        wait_bytes(got.at[k, 1, hi], rssem.at[k, 5])
        for j in range(4, 8):
            give_back(k, j)
        for j in range(4, 8):
            ship(k, j)

    def home(k):
        @pl.when(sec > 0)
        def _():
            wait_bytes(hin.at[k], hsem.at[k])

        wait_bytes(ret.at[k], retsem.at[k])
        back = ret[k].reshape(640, 128)
        update = jnp.dot(comb[k, 0], back, preferred_element_type=F32)
        update = update + jnp.dot(comb[k, 1], back, preferred_element_type=F32)
        fresh = (hin[k].astype(F32) + update).astype(BF)

        @pl.when(sec < last)
        def _():
            place_rows(place[k], fresh, dout, k)
            for e in range(8):
                send(
                    dout.at[k, e], xs.at[k, 0, me], s_disp.at[k], dsem.at[k, my_half],
                    {"pipe": sec + 1, "expert": e},
                )

        hnew[k] = fresh

        @pl.when(sec < last)
        def _():
            send(hnew.at[k], hin.at[k], s_h.at[k], hsem.at[k], {"pipe": sec + 1})

        m, half = k // 2, lax.rem(k, 2)
        mine = pl.ds(pl.multiple_of(me * 128, 128), 128)
        for i in range(4):
            owner = half * 4 + i
            block = hnew.at[k, pl.ds(i * 64, 64), :]
            place_at = outbuf.at[m, :, mine]

            @pl.when(owner == me)
            def _():
                pltpu.make_async_copy(block, place_at, osem).start()

            @pl.when(owner != me)
            def _():
                send(block, place_at, s_out.at[k, i], osem, {"expert": owner})

    def turn(k, carry):
        @pl.when(k < CHUNKS)
        def _():
            gather_start(k)
            gather_relay(k)

        @pl.when(k > 0)
        def _():
            home(k - 1)

        @pl.when(k < CHUNKS)
        def _():
            feed_forward(k)
            sum_start(k)
            sum_relay(k)
            sum_end(k)

        return carry

    lax.fori_loop(0, CHUNKS + 1, turn, 0)

    for o in range(7):
        wait_bytes(table, s_tab.at[o])

    @pl.when(sec > 0)
    def _():
        for e in range(8):
            wait_bytes(table, s_tab.at[7 + e])

    @pl.when(sec == 0)
    def _():
        for m in range(2):
            for o in range(7):
                wait_bytes(hin.at[m, pl.ds(0, 64), :], s_tok.at[m, o])
        for k in range(CHUNKS):
            wait_bytes(dfirst.at[k, pl.ds(0, 7)], s_first.at[k])

    def drain(k, carry):
        wait_bytes(xs.at[k, pl.ds(0, 3)], s_ag.at[k])
        wait_bytes(xs.at[k, pl.ds(0, 3)], s_rs.at[k])
        wait_bytes(ret.at[k, pl.ds(0, 7)], s_ret.at[k])

        @pl.when(sec < last)
        def _():
            wait_bytes(dout.at[k], s_disp.at[k])
            wait_bytes(hnew.at[k], s_h.at[k])

        for i in range(4):
            owner = lax.rem(k, 2) * 4 + i

            @pl.when(owner != me)
            def _():
                wait_bytes(hnew.at[k, pl.ds(i * 64, 64), :], s_out.at[k, i])

        return carry

    lax.fori_loop(0, CHUNKS, drain, 0)
    wait_bytes(outbuf, osem)
    final = pltpu.make_async_copy(outbuf, out, wsem.at[0])
    final.start()
    final.wait()


def local(tokens, gains, route_ids, route_weights, picks, w_gate, w_up, w_down):
    vmem = pl.BlockSpec(memory_space=pltpu.VMEM)
    anywhere = pl.BlockSpec(memory_space=pl.ANY)
    dma = pltpu.SemaphoreType.DMA
    out = pl.pallas_call(
        relay_kernel,
        name="relay",
        out_shape=jax.ShapeDtypeStruct((2, 64, 1024), BF),
        in_specs=[anywhere, vmem, vmem, vmem, vmem, anywhere, anywhere, anywhere],
        out_specs=anywhere,
        scratch_shapes=[
            pltpu.VMEM((4, 1024, 768), BF),
            pltpu.VMEM((4, 384, 1024), BF),
            pltpu.VMEM((8, 256), F32),
            pltpu.VMEM((2, 8, 8, 256), F32),
            pltpu.VMEM((CHUNKS, 640, 256), BF),
            pltpu.VMEM((CHUNKS, 2, 256, 640), BF),
            pltpu.VMEM((CHUNKS, 256, 128), BF),
            pltpu.VMEM((CHUNKS, 256, 128), BF),
            pltpu.VMEM((CHUNKS, 4, 8, 80, 128), BF),
            pltpu.VMEM((CHUNKS, 8, 80, 128), BF),
            pltpu.VMEM((CHUNKS, 8, 80, 128), BF),
            pltpu.VMEM((80, 768), F32),
            pltpu.VMEM((80, 128), F32),
            pltpu.VMEM((80, 384), BF),
            pltpu.VMEM((CHUNKS, 8, 80, 128), BF),
            pltpu.VMEM((CHUNKS, 2, 8, 80, 128), BF),
            pltpu.VMEM((CHUNKS, 2, 4, 80, 128), BF),
            pltpu.VMEM((CHUNKS, 2, 8, 80, 128), BF),
            pltpu.VMEM((CHUNKS, 8, 80, 128), BF),
            pltpu.VMEM((CHUNKS, 8, 80, 128), BF),
            pltpu.VMEM((2, 64, 1024), BF),
            dma((12,)),
            dma((2,)),
            dma((CHUNKS,)),
            dma((CHUNKS, 2)),
            dma((CHUNKS, 6)),
            dma((CHUNKS, 6)),
            dma((CHUNKS,)),
            dma(()),
            dma((15,)),
            dma((2, 7)),
            dma((CHUNKS,)),
            dma((CHUNKS,)),
            dma((CHUNKS,)),
            dma((CHUNKS,)),
            dma((CHUNKS,)),
            dma((CHUNKS,)),
            dma((CHUNKS, 4)),
        ],
        compiler_params=pltpu.CompilerParams(
            collective_id=0, has_side_effects=True, vmem_limit_bytes=56 * 1024 * 1024
        ),
    )(
        tokens, gains, jnp.swapaxes(route_ids[0], 1, 2), jnp.swapaxes(route_weights[0], 1, 2),
        picks[0, :, 0], w_gate[0, 0], w_up[0, 0], w_down[0, 0],
    )
    return out[None]


def solution(mesh):
    return jax.shard_map(
        local,
        mesh=mesh,
        in_specs=(
            P(None, "expert", None),
            P("pipe", None),
            P("pipe", None, "expert", None),
            P("pipe", None, "expert", None),
            P("pipe", None, "expert", None),
            P("pipe", "expert", None, "tensor"),
            P("pipe", "expert", None, "tensor"),
            P("pipe", "expert", "tensor", None),
        ),
        out_specs=P("pipe", None, "expert", "tensor"),
        check_vma=False,
    )
```

time: 356 us -> 318 us (0.89)
  blocking collectives: 18.2 us -> 0 us
  Pallas kernels: 324 us -> 316 us
  local copies, waits for them, and re-layouts: 6.39 us -> 1.67 us
  other arithmetic: 3.84 us -> 0 us
    all_gather x1 -> x0, blocking collectives: 18.2 us -> none  [local(): every = lax.all_gather(jnp.stack([mine, after]), 'expert')]
    pallas_call x1, Pallas kernels: 324 us -> 316 us  [local(): pl.pallas_call(relay_kernel, name='relay', out_shape=jax.ShapeDtypeStruct...]
  transfers between devices with their start and end apart: 1 -> 0, of which waited for: 0 -> 0; matrix products, arithmetic and copies ran while one was open for 1% -> 0% of each run, Pallas kernels for 0% -> 0%
where the time goes in v2:
time: 318 us; the launch traced here: 317 us
  Pallas kernels  316 us (99%)
    pallas_call x1, Pallas kernels, local(): pl.pallas_call(relay_kernel, name='relay', out_shape=jax.ShapeDtypeStruct...  316 us

profile of v2, /device:TPU:38, one launch (start us, length us, event | category | flops | bytes accessed | tf_op | source)
XLA Modules:
  0.0 317.4 jit_solution(11742052058827635402)
XLA Ops:
  0.0 315.8 %relay.1 = bf16[2,64,1024]{2,1,0:T(8,128)(2,1)} custom-call(bf16[2,64,4096]{2,1,0:T(8,128)(2,1)} %tokens.1, f32[1,4096]{1,0:T(1,128)} %gains.1, s32[2,2,64]{2,1,0:T(2,128)} %bitcast.15, f32[2,2,64]{2,1,0:T(2,128)} %bitcast.16, s32[2,64]{1,0:T(2,128)} %bitcast.17, bf16[4096,384]{1,0:T(8,128)(2,1)} %bitcast.11, bf16[4096,384]{1,0:T(8,128)(2,1)} %bitcast.12, ...), custom_call_target="tpu_custom_call" | custom-call | tf_op jit(solution)/shard_map/relay/pallas_call | solution.py:416
  315.8 1.7 copy.10

commit v3 on v2

--- a/solution.py
+++ b/solution.py
@@ -11,6 +11,8 @@
 F32 = jnp.float32
 CHUNKS = 4
 CAP = 5
+PIECE = 1
+PARTS = 4 // PIECE
 
 
 def wait_bytes(ref, sem):
@@ -32,6 +34,7 @@
     dn1 = lax.rem(rank + 3, 4)
     far = lax.rem(rank + 2, 4)
     my_half = me // 4
+    my_piece = me // PIECE
 
     def send(src, dst, ssem, rsem, dev):
         pltpu.make_async_remote_copy(
@@ -158,45 +161,48 @@
         for e in range(8):
             dest[k, e] = moved[e * 80 : (e + 1) * 80]
 
-    wait_bytes(tables.at[0], tsem.at[0])
+    def first(k):
+        place_rows(placing(0, k), hin[k], dfirst, k)
+        for o in range(1, 8):
+            e = lax.rem(me + o, 8)
+            send(dfirst.at[k, e], xs.at[k, 0, me], s_first.at[k], dsem.at[k, my_piece], {"expert": e})
+        pltpu.make_async_copy(dfirst.at[k, me], xs.at[k, 0, me], dsem.at[k, my_piece]).start()
 
     @pl.when(sec == 0)
     def _():
-        def first(k, carry):
-            matrix = placing(0, k)
-            wait_bytes(hin.at[k], hsem.at[k])
-            place_rows(matrix, hin[k], dfirst, k)
-            for o in range(1, 8):
-                e = lax.rem(me + o, 8)
-                send(dfirst.at[k, e], xs.at[k, 0, me], s_first.at[k], dsem.at[k, my_half], {"expert": e})
-            pltpu.make_async_copy(dfirst.at[k, me], xs.at[k, 0, me], dsem.at[k, my_half]).start()
-            return carry
-
-        lax.fori_loop(0, CHUNKS, first, 0)
-
-    def build(k, carry):
+        wait_bytes(tables.at[0], tsem.at[0])
+        wait_bytes(hin.at[0], hsem.at[0])
+        first(0)
+
+    def prepare(k):
+        @pl.when((k < CHUNKS - 1) & (sec == 0))
+        def _():
+            wait_bytes(hin.at[k + 1], hsem.at[k + 1])
+            first(k + 1)
+
+        @pl.when((k == 0) & (sec > 0))
+        def _():
+            wait_bytes(tables.at[0], tsem.at[0])
+
+        @pl.when((k == 0) & (sec < last))
+        def _():
+            wait_bytes(tables.at[1], tsem.at[1])
+
         cols = [column(row, eye256) for row in fields(0, k, (0, 1, 2, 3))]
         mix = jnp.where(slot_cols == cols[0], cols[2], 0.0)
         mix = mix + jnp.where(slot_cols == cols[1], cols[3], 0.0)
         high = mix.astype(BF)
         comb[k, 0] = high
         comb[k, 1] = (mix - high.astype(F32)).astype(BF)
-        return carry
-
-    lax.fori_loop(0, CHUNKS, build, 0)
-
-    @pl.when(sec < last)
-    def _():
-        wait_bytes(tables.at[1], tsem.at[1])
-
-        def build_next(k, carry):
+
+        @pl.when(sec < last)
+        def _():
             place[k] = placing(1, k)
-            return carry
-
-        lax.fori_loop(0, CHUNKS, build_next, 0)
-
-    for copy in weight_copies():
-        copy.wait()
+
+        @pl.when(k == 0)
+        def _():
+            for copy in weight_copies():
+                copy.wait()
 
     lo, hi = pl.ds(0, 4), pl.ds(4, 4)
     to_up, to_dn = {"tensor": up1}, {"tensor": dn1}
@@ -210,35 +216,45 @@
         both = jnp.dot(scaled.astype(BF), wgu[origin], preferred_element_type=F32)
         return jnp.sum(x * x, axis=1, keepdims=True), both
 
+    def low(p):
+        return pl.ds(p * PIECE, PIECE)
+
+    def high_of(p):
+        return pl.ds(4 + p * PIECE, PIECE)
+
     def gather_start(k):
         ssem = s_ag.at[k]
-        wait_bytes(xs.at[k, 0, lo], dsem.at[k, 0])
-        send(xs.at[k, 0, lo], xs.at[k, 1, lo], ssem, agsem.at[k, 0], to_up)
-        wait_bytes(xs.at[k, 0, hi], dsem.at[k, 1])
-        send(xs.at[k, 0, hi], xs.at[k, 2, hi], ssem, agsem.at[k, 1], to_dn)
-        send(xs.at[k, 0, lo], xs.at[k, 2, lo], ssem, agsem.at[k, 2], to_dn)
-        send(xs.at[k, 0, hi], xs.at[k, 1, hi], ssem, agsem.at[k, 3], to_up)
+        for p in range(PARTS):
+            wait_bytes(xs.at[k, 0, low(p)], dsem.at[k, p])
+            send(xs.at[k, 0, low(p)], xs.at[k, 1, low(p)], ssem, agsem.at[k, p], to_up)
+        for p in range(PARTS):
+            wait_bytes(xs.at[k, 0, high_of(p)], dsem.at[k, PARTS + p])
+            send(xs.at[k, 0, high_of(p)], xs.at[k, 2, high_of(p)], ssem, agsem.at[k, PARTS + p], to_dn)
+        send(xs.at[k, 0, lo], xs.at[k, 2, lo], ssem, agsem.at[k, 4 * PARTS], to_dn)
+        send(xs.at[k, 0, hi], xs.at[k, 1, hi], ssem, agsem.at[k, 4 * PARTS + 1], to_up)
 
     def gather_relay(k):
         ssem = s_ag.at[k]
         sq, both = part(k, 0, rank)
         acc[...] = both
         squares[...] = jnp.broadcast_to(sq, (80, 128))
-        wait_bytes(xs.at[k, 1, lo], agsem.at[k, 0])
-        send(xs.at[k, 1, lo], xs.at[k, 3, lo], ssem, agsem.at[k, 4], to_up)
-        wait_bytes(xs.at[k, 2, hi], agsem.at[k, 1])
-        send(xs.at[k, 2, hi], xs.at[k, 3, hi], ssem, agsem.at[k, 5], to_dn)
+        for p in range(PARTS):
+            wait_bytes(xs.at[k, 1, low(p)], agsem.at[k, p])
+            send(xs.at[k, 1, low(p)], xs.at[k, 3, low(p)], ssem, agsem.at[k, 2 * PARTS + p], to_up)
+            wait_bytes(xs.at[k, 2, high_of(p)], agsem.at[k, PARTS + p])
+            send(xs.at[k, 2, high_of(p)], xs.at[k, 3, high_of(p)], ssem, agsem.at[k, 3 * PARTS + p], to_dn)
 
     def feed_forward(k):
         both, sq = acc[...], squares[:, 0:1]
-        wait_bytes(xs.at[k, 1, hi], agsem.at[k, 3])
+        wait_bytes(xs.at[k, 1, hi], agsem.at[k, 4 * PARTS + 1])
         s, b = part(k, 1, dn1)
         sq, both = sq + s, both + b
-        wait_bytes(xs.at[k, 2, lo], agsem.at[k, 2])
+        wait_bytes(xs.at[k, 2, lo], agsem.at[k, 4 * PARTS])
         s, b = part(k, 2, up1)
         sq, both = sq + s, both + b
-        wait_bytes(xs.at[k, 3, lo], agsem.at[k, 4])
-        wait_bytes(xs.at[k, 3, hi], agsem.at[k, 5])
+        for p in range(PARTS):
+            wait_bytes(xs.at[k, 3, low(p)], agsem.at[k, 2 * PARTS + p])
+            wait_bytes(xs.at[k, 3, high_of(p)], agsem.at[k, 3 * PARTS + p])
         s, b = part(k, 3, far)
         sq, both = sq + s, both + b
         both = both * lax.rsqrt(sq * (1.0 / 4096.0) + EPS)
@@ -253,30 +269,32 @@
         value = down(far)
         for j in range(8):
             opp[k, j] = lanes(value, j)
-        send(opp.at[k, lo], relay.at[k, 0], ssem, rssem.at[k, 0], to_up)
-        send(opp.at[k, hi], relay.at[k, 1], ssem, rssem.at[k, 1], to_dn)
+        for p in range(PARTS):
+            send(opp.at[k, low(p)], relay.at[k, 0, low(p)], ssem, rssem.at[k, p], to_up)
+            send(opp.at[k, high_of(p)], relay.at[k, 1, low(p)], ssem, rssem.at[k, PARTS + p], to_dn)
         value = down(up1)
         for j in range(8):
             side[k, 0, j] = lanes(value, j)
-        send(side.at[k, 0, hi], got.at[k, 0, hi], ssem, rssem.at[k, 2], to_up)
+        send(side.at[k, 0, hi], got.at[k, 0, hi], ssem, rssem.at[k, 4 * PARTS], to_up)
         value = down(dn1)
         for j in range(8):
             side[k, 1, j] = lanes(value, j)
-        send(side.at[k, 1, lo], got.at[k, 1, lo], ssem, rssem.at[k, 3], to_dn)
+        send(side.at[k, 1, lo], got.at[k, 1, lo], ssem, rssem.at[k, 4 * PARTS + 1], to_dn)
         value = down(rank)
         for j in range(8):
             rout[k, j] = lanes(value, j)
 
     def sum_relay(k):
         ssem = s_rs.at[k]
-        wait_bytes(relay.at[k, 0], rssem.at[k, 0])
-        for j in range(4):
-            side[k, 0, j] = (side[k, 0, j].astype(F32) + relay[k, 0, j].astype(F32)).astype(BF)
-        send(side.at[k, 0, lo], got.at[k, 0, lo], ssem, rssem.at[k, 4], to_up)
-        wait_bytes(relay.at[k, 1], rssem.at[k, 1])
-        for j in range(4, 8):
-            side[k, 1, j] = (side[k, 1, j].astype(F32) + relay[k, 1, j - 4].astype(F32)).astype(BF)
-        send(side.at[k, 1, hi], got.at[k, 1, hi], ssem, rssem.at[k, 5], to_dn)
+        for p in range(PARTS):
+            wait_bytes(relay.at[k, 0, low(p)], rssem.at[k, p])
+            for j in range(p * PIECE, (p + 1) * PIECE):
+                side[k, 0, j] = (side[k, 0, j].astype(F32) + relay[k, 0, j].astype(F32)).astype(BF)
+            send(side.at[k, 0, low(p)], got.at[k, 0, low(p)], ssem, rssem.at[k, 2 * PARTS + p], to_up)
+            wait_bytes(relay.at[k, 1, low(p)], rssem.at[k, PARTS + p])
+            for j in range(p * PIECE, (p + 1) * PIECE):
+                side[k, 1, 4 + j] = (side[k, 1, 4 + j].astype(F32) + relay[k, 1, j].astype(F32)).astype(BF)
+            send(side.at[k, 1, high_of(p)], got.at[k, 1, high_of(p)], ssem, rssem.at[k, 3 * PARTS + p], to_dn)
 
     def give_back(k, j):
         total = rout[k, j].astype(F32) + got[k, 0, j].astype(F32) + got[k, 1, j].astype(F32)
@@ -292,18 +310,15 @@
             send(rout.at[k, j], ret.at[k, me], s_ret.at[k], retsem.at[k], {"expert": j})
 
     def sum_end(k):
-        wait_bytes(got.at[k, 1, lo], rssem.at[k, 3])
-        wait_bytes(got.at[k, 0, lo], rssem.at[k, 4])
-        for j in range(4):
-            give_back(k, j)
-        for j in range(4):
-            ship(k, j)
-        wait_bytes(got.at[k, 0, hi], rssem.at[k, 2])
-        wait_bytes(got.at[k, 1, hi], rssem.at[k, 5])
-        for j in range(4, 8):
-            give_back(k, j)
-        for j in range(4, 8):
-            ship(k, j)
+        wait_bytes(got.at[k, 1, lo], rssem.at[k, 4 * PARTS + 1])
+        wait_bytes(got.at[k, 0, hi], rssem.at[k, 4 * PARTS])
+        for p in range(PARTS):
+            for begin, which in ((p * PIECE, 0), (4 + p * PIECE, 1)):
+                wait_bytes(got.at[k, which, pl.ds(begin, PIECE)], rssem.at[k, (2 + which) * PARTS + p])
+                for j in range(begin, begin + PIECE):
+                    give_back(k, j)
+                for j in range(begin, begin + PIECE):
+                    ship(k, j)
 
     def home(k):
         @pl.when(sec > 0)
@@ -321,7 +336,7 @@
             place_rows(place[k], fresh, dout, k)
             for e in range(8):
                 send(
-                    dout.at[k, e], xs.at[k, 0, me], s_disp.at[k], dsem.at[k, my_half],
+                    dout.at[k, e], xs.at[k, 0, me], s_disp.at[k], dsem.at[k, my_piece],
                     {"pipe": sec + 1, "expert": e},
                 )
 
@@ -347,21 +362,28 @@
                 send(block, place_at, s_out.at[k, i], osem, {"expert": owner})
 
     def turn(k, carry):
-        @pl.when(k < CHUNKS)
+        @pl.when((k < CHUNKS))
         def _():
             gather_start(k)
+            prepare(k)
+
+        @pl.when((k >= 1))
+        def _():
+            sum_end(k - 1)
+
+        @pl.when((k < CHUNKS))
+        def _():
             gather_relay(k)
 
-        @pl.when(k > 0)
+        @pl.when((k >= 1))
         def _():
             home(k - 1)
 
-        @pl.when(k < CHUNKS)
+        @pl.when((k < CHUNKS))
         def _():
             feed_forward(k)
             sum_start(k)
             sum_relay(k)
-            sum_end(k)
 
         return carry
 
@@ -444,9 +466,9 @@
             dma((12,)),
             dma((2,)),
             dma((CHUNKS,)),
-            dma((CHUNKS, 2)),
-            dma((CHUNKS, 6)),
-            dma((CHUNKS, 6)),
+            dma((CHUNKS, 2 * PARTS)),
+            dma((CHUNKS, 4 * PARTS + 2)),
+            dma((CHUNKS, 4 * PARTS + 2)),
             dma((CHUNKS,)),
             dma(()),
             dma((15,)),

time: 318 us -> 299 us (0.940)
  Pallas kernels: 316 us -> 297 us
    pallas_call x1, Pallas kernels: 316 us -> 297 us  [local(): pl.pallas_call(relay_kernel, name='relay', out_shape=jax.ShapeDtypeStruct...]
where the time goes in v3:
time: 299 us; the launch traced here: 298 us
  Pallas kernels  297 us (99%)
    pallas_call x1, Pallas kernels, local(): pl.pallas_call(relay_kernel, name='relay', out_shape=jax.ShapeDtypeStruct...  297 us

profile of v3, /device:TPU:38, one launch (start us, length us, event | category | flops | bytes accessed | tf_op | source)
XLA Modules:
  0.0 298.2 jit_solution(3585936466385204849)
XLA Ops:
  0.0 296.5 %relay.1 = bf16[2,64,1024]{2,1,0:T(8,128)(2,1)} custom-call(bf16[2,64,4096]{2,1,0:T(8,128)(2,1)} %tokens.1, f32[1,4096]{1,0:T(1,128)} %gains.1, s32[2,2,64]{2,1,0:T(2,128)} %bitcast.15, f32[2,2,64]{2,1,0:T(2,128)} %bitcast.16, s32[2,64]{1,0:T(2,128)} %bitcast.17, bf16[4096,384]{1,0:T(8,128)(2,1)} %bitcast.11, bf16[4096,384]{1,0:T(8,128)(2,1)} %bitcast.12, ...), custom_call_target="tpu_custom_call" | custom-call | tf_op jit(solution)/shard_map/relay/pallas_call | solution.py:438
  296.5 1.7 copy.10

commit v4 on v3

--- a/solution.py
+++ b/solution.py
@@ -21,10 +21,10 @@
 
 def relay_kernel(
     tokens, gains, ids, route_w, picks, w_gate, w_up, w_down, out,
-    wgu, wd, table, tables, place, comb, hin, hnew, xs, dfirst, dout, acc, squares, hid,
+    wgu, wd, table, tables, place, comb, hin, hnew, xs, dfirst, dout, acc, squares, hid, total, relay_w,
     opp, side, relay, got, rout, ret, outbuf,
-    wsem, tsem, hsem, dsem, agsem, rssem, retsem, osem,
-    s_tab, s_tok, s_first, s_disp, s_ag, s_rs, s_ret, s_h, s_out,
+    wsem, dwsem, tsem, hsem, dsem, agsem, rssem, retsem, osem,
+    s_tab, s_dw, s_tok, s_first, s_disp, s_ag, s_rs, s_ret, s_h, s_out,
 ):
     sec = lax.axis_index("pipe")
     rank = lax.axis_index("tensor")
@@ -51,6 +51,7 @@
         greet({"expert": lax.rem(me + o, 8)})
     greet({"tensor": up1})
     greet({"tensor": dn1})
+    greet({"tensor": far})
 
     @pl.when(sec < last)
     def _():
@@ -67,12 +68,28 @@
         for q in range(4):
             copies.append((w_gate.at[pl.ds(q * 1024, 1024), :], wgu.at[q, :, pl.ds(0, 384)]))
             copies.append((w_up.at[pl.ds(q * 1024, 1024), :], wgu.at[q, :, pl.ds(384, 384)]))
-        for q in range(4):
-            copies.append((w_down.at[:, pl.ds(q * 1024, 1024)], wd.at[q]))
         return [pltpu.make_async_copy(a, b, wsem.at[i]) for i, (a, b) in enumerate(copies)]
+
+    def slice_of_down(q):
+        return w_down.at[:, pl.ds(pl.multiple_of(q * 1024, 128), 1024)]
+
+    def first_down_copies():
+        return [pltpu.make_async_copy(slice_of_down(q), wd.at[q], wsem.at[8 + q]) for q in range(4)]
+
+    def own_down_copy():
+        return pltpu.make_async_copy(slice_of_down(rank), wd.at[rank], wsem.at[8])
 
     for copy in weight_copies():
         copy.start()
+
+    @pl.when(sec == 0)
+    def _():
+        for copy in first_down_copies():
+            copy.start()
+
+    @pl.when(sec > 0)
+    def _():
+        own_down_copy().start()
 
     def iota(shape, dim):
         return lax.broadcasted_iota(jnp.int32, shape, dim).astype(F32)
@@ -107,7 +124,7 @@
                 whole = whole + jnp.where(row_of == m * 4 + field, placed, 0.0)
     table[...] = whole
 
-    greeted = 9 + jnp.where(sec < last, 8, 0) + jnp.where(sec > 0, 8, 0)
+    greeted = 10 + jnp.where(sec < last, 8, 0) + jnp.where(sec > 0, 8, 0)
     pl.semaphore_wait(barrier, greeted)
 
     @pl.when(sec == 0)
@@ -137,6 +154,21 @@
         for e in range(8):
             send(table, tables.at[1, me], s_tab.at[7 + e], tsem.at[1], {"pipe": sec - 1, "expert": e})
 
+    to_up, to_dn = {"tensor": up1}, {"tensor": dn1}
+    top, rest = pl.ds(0, 192), pl.ds(192, 192)
+
+    @pl.when(sec > 0)
+    def _():
+        distant = pl.ds(pl.multiple_of(far * 1024, 128), 1024)
+        send(w_down.at[top, distant], relay_w.at[0], s_dw.at[0], dwsem.at[2], to_up)
+        send(w_down.at[rest, distant], relay_w.at[1], s_dw.at[1], dwsem.at[3], to_dn)
+        send(slice_of_down(up1), wd.at[rank], s_dw.at[2], dwsem.at[0], to_up)
+        send(slice_of_down(dn1), wd.at[rank], s_dw.at[3], dwsem.at[1], to_dn)
+        wait_bytes(relay_w.at[0], dwsem.at[2])
+        send(relay_w.at[0], wd.at[dn1, top], s_dw.at[4], dwsem.at[4], to_up)
+        wait_bytes(relay_w.at[1], dwsem.at[3])
+        send(relay_w.at[1], wd.at[up1, rest], s_dw.at[5], dwsem.at[5], to_dn)
+
     slot_rows = iota((640, 256), 0)
     slot_cols = iota((256, 640), 1)
     eye256 = iota((256, 256), 0) == iota((256, 256), 1)
@@ -204,8 +236,20 @@
             for copy in weight_copies():
                 copy.wait()
 
+        @pl.when((k == 0) & (sec == 0))
+        def _():
+            for copy in first_down_copies():
+                copy.wait()
+
+        @pl.when((k == 0) & (sec > 0))
+        def _():
+            own_down_copy().wait()
+            wait_bytes(wd.at[dn1], dwsem.at[0])
+            wait_bytes(wd.at[up1], dwsem.at[1])
+            wait_bytes(wd.at[far, top], dwsem.at[4])
+            wait_bytes(wd.at[far, rest], dwsem.at[5])
+
     lo, hi = pl.ds(0, 4), pl.ds(4, 4)
-    to_up, to_dn = {"tensor": up1}, {"tensor": dn1}
 
     def lanes(value, j):
         return value[:, j * 128 : (j + 1) * 128]
@@ -259,32 +303,51 @@
         sq, both = sq + s, both + b
         both = both * lax.rsqrt(sq * (1.0 / 4096.0) + EPS)
         gate, up = both[:, :384], both[:, 384:]
-        hid[...] = (gate / (1.0 + jnp.exp(-gate)) * up).astype(BF)
-
-    def down(q):
-        return jnp.dot(hid[...], wd[q], preferred_element_type=F32).astype(BF)
-
-    def sum_start(k):
+        hid[k, 0] = (gate / (1.0 + jnp.exp(-gate)) * up).astype(BF)
+
+    def down(k, q):
+        return jnp.dot(hid[k, 0], wd[q], preferred_element_type=F32).astype(BF)
+
+    def spread_start(k):
         ssem = s_rs.at[k]
-        value = down(far)
+        send(hid.at[k, 0], hid.at[k, 3], ssem, rssem.at[k, 2], {"tensor": far})
+        send(hid.at[k, 0], hid.at[k, 1], ssem, rssem.at[k, 0], to_up)
+        send(hid.at[k, 0], hid.at[k, 2], ssem, rssem.at[k, 1], to_dn)
+        total[...] = jnp.dot(hid[k, 0], wd[rank], preferred_element_type=F32)
+
+    def spread_end(k):
+        wait_bytes(hid.at[k, 1], rssem.at[k, 0])
+        total[...] += jnp.dot(hid[k, 1], wd[dn1], preferred_element_type=F32)
+        wait_bytes(hid.at[k, 2], rssem.at[k, 1])
+        total[...] += jnp.dot(hid[k, 2], wd[up1], preferred_element_type=F32)
+        wait_bytes(hid.at[k, 3], rssem.at[k, 2])
+        done = (total[...] + jnp.dot(hid[k, 3], wd[far], preferred_element_type=F32)).astype(BF)
+        for j in range(8):
+            rout[k, j] = lanes(done, j)
+        for j in range(8):
+            ship(k, j)
+
+    def first_layer_sum_start(k):
+        ssem = s_rs.at[k]
+        value = down(k, far)
         for j in range(8):
             opp[k, j] = lanes(value, j)
         for p in range(PARTS):
             send(opp.at[k, low(p)], relay.at[k, 0, low(p)], ssem, rssem.at[k, p], to_up)
             send(opp.at[k, high_of(p)], relay.at[k, 1, low(p)], ssem, rssem.at[k, PARTS + p], to_dn)
-        value = down(up1)
+        value = down(k, up1)
         for j in range(8):
             side[k, 0, j] = lanes(value, j)
         send(side.at[k, 0, hi], got.at[k, 0, hi], ssem, rssem.at[k, 4 * PARTS], to_up)
-        value = down(dn1)
+        value = down(k, dn1)
         for j in range(8):
             side[k, 1, j] = lanes(value, j)
         send(side.at[k, 1, lo], got.at[k, 1, lo], ssem, rssem.at[k, 4 * PARTS + 1], to_dn)
-        value = down(rank)
+        value = down(k, rank)
         for j in range(8):
             rout[k, j] = lanes(value, j)
 
-    def sum_relay(k):
+    def first_layer_sum_relay(k):
         ssem = s_rs.at[k]
         for p in range(PARTS):
             wait_bytes(relay.at[k, 0, low(p)], rssem.at[k, p])
@@ -309,7 +372,7 @@
         def _():
             send(rout.at[k, j], ret.at[k, me], s_ret.at[k], retsem.at[k], {"expert": j})
 
-    def sum_end(k):
+    def first_layer_sum_end(k):
         wait_bytes(got.at[k, 1, lo], rssem.at[k, 4 * PARTS + 1])
         wait_bytes(got.at[k, 0, hi], rssem.at[k, 4 * PARTS])
         for p in range(PARTS):
@@ -320,6 +383,29 @@
                 for j in range(begin, begin + PIECE):
                     ship(k, j)
 
+    def sum_start(k):
+        @pl.when(sec == 0)
+        def _():
+            first_layer_sum_start(k)
+
+        @pl.when(sec > 0)
+        def _():
+            spread_start(k)
+
+    def sum_relay(k):
+        @pl.when(sec == 0)
+        def _():
+            first_layer_sum_relay(k)
+
+    def sum_end(k):
+        @pl.when(sec == 0)
+        def _():
+            first_layer_sum_end(k)
+
+        @pl.when(sec > 0)
+        def _():
+            spread_end(k)
+
     def home(k):
         @pl.when(sec > 0)
         def _():
@@ -366,13 +452,6 @@
         def _():
             gather_start(k)
             prepare(k)
-
-        @pl.when((k >= 1))
-        def _():
-            sum_end(k - 1)
-
-        @pl.when((k < CHUNKS))
-        def _():
             gather_relay(k)
 
         @pl.when((k >= 1))
@@ -384,6 +463,7 @@
             feed_forward(k)
             sum_start(k)
             sum_relay(k)
+            sum_end(k)
 
         return carry
 
@@ -396,6 +476,10 @@
     def _():
         for e in range(8):
             wait_bytes(table, s_tab.at[7 + e])
+        for i in range(4):
+            wait_bytes(relay_w.at[0] if i < 2 else wd.at[0], s_dw.at[i])
+        for i in range(2):
+            wait_bytes(relay_w.at[i], s_dw.at[4 + i])
 
     @pl.when(sec == 0)
     def _():
@@ -407,7 +491,15 @@
 
     def drain(k, carry):
         wait_bytes(xs.at[k, pl.ds(0, 3)], s_ag.at[k])
-        wait_bytes(xs.at[k, pl.ds(0, 3)], s_rs.at[k])
+
+        @pl.when(sec == 0)
+        def _():
+            wait_bytes(xs.at[k, pl.ds(0, 3)], s_rs.at[k])
+
+        @pl.when(sec > 0)
+        def _():
+            wait_bytes(hid.at[k, pl.ds(0, 3)], s_rs.at[k])
+
         wait_bytes(ret.at[k, pl.ds(0, 7)], s_ret.at[k])
 
         @pl.when(sec < last)
@@ -455,7 +547,9 @@
             pltpu.VMEM((CHUNKS, 8, 80, 128), BF),
             pltpu.VMEM((80, 768), F32),
             pltpu.VMEM((80, 128), F32),
-            pltpu.VMEM((80, 384), BF),
+            pltpu.VMEM((CHUNKS, 4, 80, 384), BF),
+            pltpu.VMEM((80, 1024), F32),
+            pltpu.VMEM((2, 192, 1024), BF),
             pltpu.VMEM((CHUNKS, 8, 80, 128), BF),
             pltpu.VMEM((CHUNKS, 2, 8, 80, 128), BF),
             pltpu.VMEM((CHUNKS, 2, 4, 80, 128), BF),
@@ -464,6 +558,7 @@
             pltpu.VMEM((CHUNKS, 8, 80, 128), BF),
             pltpu.VMEM((2, 64, 1024), BF),
             dma((12,)),
+            dma((6,)),
             dma((2,)),
             dma((CHUNKS,)),
             dma((CHUNKS, 2 * PARTS)),
@@ -472,6 +567,7 @@
             dma((CHUNKS,)),
             dma(()),
             dma((15,)),
+            dma((6,)),
             dma((2, 7)),
             dma((CHUNKS,)),
             dma((CHUNKS,)),

time: 299 us -> 283 us (0.946)
  Pallas kernels: 297 us -> 281 us
    pallas_call x1, Pallas kernels: 297 us -> 281 us  [local(): pl.pallas_call(relay_kernel, name='relay', out_shape=jax.ShapeDtypeStruct...]
where the time goes in v4:
time: 283 us
  Pallas kernels  281 us (99%)
    pallas_call x1, Pallas kernels, local(): pl.pallas_call(relay_kernel, name='relay', out_shape=jax.ShapeDtypeStruct...  281 us

profile of v4, /device:TPU:38, one launch (start us, length us, event | category | flops | bytes accessed | tf_op | source)
XLA Modules:
  0.0 282.6 jit_solution(5525718493249517929)
XLA Ops:
  0.0 280.9 %relay.1 = bf16[2,64,1024]{2,1,0:T(8,128)(2,1)} custom-call(bf16[2,64,4096]{2,1,0:T(8,128)(2,1)} %tokens.1, f32[1,4096]{1,0:T(1,128)} %gains.1, s32[2,2,64]{2,1,0:T(2,128)} %bitcast.15, f32[2,2,64]{2,1,0:T(2,128)} %bitcast.16, s32[2,64]{1,0:T(2,128)} %bitcast.17, bf16[4096,384]{1,0:T(8,128)(2,1)} %bitcast.11, bf16[4096,384]{1,0:T(8,128)(2,1)} %bitcast.12, ...), custom_call_target="tpu_custom_call" | custom-call | tf_op jit(solution)/shard_map/relay/pallas_call | solution.py:530
  281.0 1.7 copy.10

commit v5 on v4

--- a/solution.py
+++ b/solution.py
@@ -11,8 +11,7 @@
 F32 = jnp.float32
 CHUNKS = 4
 CAP = 5
-PIECE = 1
-PARTS = 4 // PIECE
+PARTS = 4
 
 
 def wait_bytes(ref, sem):
@@ -34,7 +33,9 @@
     dn1 = lax.rem(rank + 3, 4)
     far = lax.rem(rank + 2, 4)
     my_half = me // 4
-    my_piece = me // PIECE
+    chip, core = me // 2, lax.rem(me, 2)
+    partner = chip * 2 + 1 - core
+    my_piece = core * 4 + chip
 
     def send(src, dst, ssem, rsem, dev):
         pltpu.make_async_remote_copy(
@@ -127,6 +128,15 @@
     greeted = 10 + jnp.where(sec < last, 8, 0) + jnp.where(sec > 0, 8, 0)
     pl.semaphore_wait(barrier, greeted)
 
+    for o in range(1, 8):
+        send(table, tables.at[0, me], s_tab.at[o - 1], tsem.at[0], {"expert": lax.rem(me + o, 8)})
+    pltpu.make_async_copy(table, tables.at[0, me], tsem.at[0]).start()
+
+    @pl.when(sec > 0)
+    def _():
+        for e in range(8):
+            send(table, tables.at[1, me], s_tab.at[7 + e], tsem.at[1], {"pipe": sec - 1, "expert": e})
+
     @pl.when(sec == 0)
     def _():
         start = pl.multiple_of(rank * 1024, 128)
@@ -145,15 +155,6 @@
                 hin.at[k, pl.ds(row, 64), :], hsem.at[k],
             ).start()
 
-    for o in range(1, 8):
-        send(table, tables.at[0, me], s_tab.at[o - 1], tsem.at[0], {"expert": lax.rem(me + o, 8)})
-    pltpu.make_async_copy(table, tables.at[0, me], tsem.at[0]).start()
-
-    @pl.when(sec > 0)
-    def _():
-        for e in range(8):
-            send(table, tables.at[1, me], s_tab.at[7 + e], tsem.at[1], {"pipe": sec - 1, "expert": e})
-
     to_up, to_dn = {"tensor": up1}, {"tensor": dn1}
     top, rest = pl.ds(0, 192), pl.ds(192, 192)
 
@@ -193,12 +194,16 @@
         for e in range(8):
             dest[k, e] = moved[e * 80 : (e + 1) * 80]
 
+    def far_first(side):
+        order = [lax.rem(chip + o, 4) * 2 for o in (2, side, 4 - side)]
+        return [base + c for base in order for c in range(2)]
+
     def first(k):
         place_rows(placing(0, k), hin[k], dfirst, k)
         for o in range(1, 8):
             e = lax.rem(me + o, 8)
-            send(dfirst.at[k, e], xs.at[k, 0, me], s_first.at[k], dsem.at[k, my_piece], {"expert": e})
-        pltpu.make_async_copy(dfirst.at[k, me], xs.at[k, 0, me], dsem.at[k, my_piece]).start()
+            send(dfirst.at[k, e], xs.at[k, 0, my_piece], s_first.at[k], dsem.at[k, my_piece], {"expert": e})
+        pltpu.make_async_copy(dfirst.at[k, me], xs.at[k, 0, my_piece], dsem.at[k, my_piece]).start()
 
     @pl.when(sec == 0)
     def _():
@@ -255,23 +260,25 @@
         return value[:, j * 128 : (j + 1) * 128]
 
     def part(k, rel, origin):
-        x = jnp.concatenate([xs[k, rel, j] for j in range(8)], axis=1).astype(F32)
+        x = jnp.concatenate([xs[k, rel, (j % 2) * 4 + j // 2] for j in range(8)], axis=1).astype(F32)
         scaled = x * gains[:, pl.ds(pl.multiple_of(origin * 1024, 128), 1024)]
         both = jnp.dot(scaled.astype(BF), wgu[origin], preferred_element_type=F32)
         return jnp.sum(x * x, axis=1, keepdims=True), both
 
+    def chips():
+        return [lax.rem(chip + o, 4) for o in (0, 1, 3, 2)]
+
     def low(p):
-        return pl.ds(p * PIECE, PIECE)
+        return pl.ds(p, 1)
 
     def high_of(p):
-        return pl.ds(4 + p * PIECE, PIECE)
+        return pl.ds(4 + p, 1)
 
     def gather_start(k):
         ssem = s_ag.at[k]
-        for p in range(PARTS):
+        for p in chips():
             wait_bytes(xs.at[k, 0, low(p)], dsem.at[k, p])
             send(xs.at[k, 0, low(p)], xs.at[k, 1, low(p)], ssem, agsem.at[k, p], to_up)
-        for p in range(PARTS):
             wait_bytes(xs.at[k, 0, high_of(p)], dsem.at[k, PARTS + p])
             send(xs.at[k, 0, high_of(p)], xs.at[k, 2, high_of(p)], ssem, agsem.at[k, PARTS + p], to_dn)
         send(xs.at[k, 0, lo], xs.at[k, 2, lo], ssem, agsem.at[k, 4 * PARTS], to_dn)
@@ -282,7 +289,7 @@
         sq, both = part(k, 0, rank)
         acc[...] = both
         squares[...] = jnp.broadcast_to(sq, (80, 128))
-        for p in range(PARTS):
+        for p in chips():
             wait_bytes(xs.at[k, 1, low(p)], agsem.at[k, p])
             send(xs.at[k, 1, low(p)], xs.at[k, 3, low(p)], ssem, agsem.at[k, 2 * PARTS + p], to_up)
             wait_bytes(xs.at[k, 2, high_of(p)], agsem.at[k, PARTS + p])
@@ -324,8 +331,10 @@
         done = (total[...] + jnp.dot(hid[k, 3], wd[far], preferred_element_type=F32)).astype(BF)
         for j in range(8):
             rout[k, j] = lanes(done, j)
-        for j in range(8):
-            ship(k, j)
+        for j in far_first(1):
+            send(rout.at[k, j], ret.at[k, me], s_ret.at[k], retsem.at[k], {"expert": j})
+        send(rout.at[k, partner], ret.at[k, me], s_ret.at[k], retsem.at[k], {"expert": partner})
+        pltpu.make_async_copy(rout.at[k, me], ret.at[k, me], retsem.at[k]).start()
 
     def first_layer_sum_start(k):
         ssem = s_rs.at[k]
@@ -351,11 +360,11 @@
         ssem = s_rs.at[k]
         for p in range(PARTS):
             wait_bytes(relay.at[k, 0, low(p)], rssem.at[k, p])
-            for j in range(p * PIECE, (p + 1) * PIECE):
+            for j in range(p, p + 1):
                 side[k, 0, j] = (side[k, 0, j].astype(F32) + relay[k, 0, j].astype(F32)).astype(BF)
             send(side.at[k, 0, low(p)], got.at[k, 0, low(p)], ssem, rssem.at[k, 2 * PARTS + p], to_up)
             wait_bytes(relay.at[k, 1, low(p)], rssem.at[k, PARTS + p])
-            for j in range(p * PIECE, (p + 1) * PIECE):
+            for j in range(p, p + 1):
                 side[k, 1, 4 + j] = (side[k, 1, 4 + j].astype(F32) + relay[k, 1, j].astype(F32)).astype(BF)
             send(side.at[k, 1, high_of(p)], got.at[k, 1, high_of(p)], ssem, rssem.at[k, 3 * PARTS + p], to_dn)
 
@@ -376,12 +385,11 @@
         wait_bytes(got.at[k, 1, lo], rssem.at[k, 4 * PARTS + 1])
         wait_bytes(got.at[k, 0, hi], rssem.at[k, 4 * PARTS])
         for p in range(PARTS):
-            for begin, which in ((p * PIECE, 0), (4 + p * PIECE, 1)):
-                wait_bytes(got.at[k, which, pl.ds(begin, PIECE)], rssem.at[k, (2 + which) * PARTS + p])
-                for j in range(begin, begin + PIECE):
-                    give_back(k, j)
-                for j in range(begin, begin + PIECE):
-                    ship(k, j)
+            for which in (0, 1):
+                j = 4 * which + p
+                wait_bytes(got.at[k, which, pl.ds(j, 1)], rssem.at[k, (2 + which) * PARTS + p])
+                give_back(k, j)
+                ship(k, j)
 
     def sum_start(k):
         @pl.when(sec == 0)
@@ -406,32 +414,7 @@
         def _():
             spread_end(k)
 
-    def home(k):
-        @pl.when(sec > 0)
-        def _():
-            wait_bytes(hin.at[k], hsem.at[k])
-
-        wait_bytes(ret.at[k], retsem.at[k])
-        back = ret[k].reshape(640, 128)
-        update = jnp.dot(comb[k, 0], back, preferred_element_type=F32)
-        update = update + jnp.dot(comb[k, 1], back, preferred_element_type=F32)
-        fresh = (hin[k].astype(F32) + update).astype(BF)
-
-        @pl.when(sec < last)
-        def _():
-            place_rows(place[k], fresh, dout, k)
-            for e in range(8):
-                send(
-                    dout.at[k, e], xs.at[k, 0, me], s_disp.at[k], dsem.at[k, my_piece],
-                    {"pipe": sec + 1, "expert": e},
-                )
-
-        hnew[k] = fresh
-
-        @pl.when(sec < last)
-        def _():
-            send(hnew.at[k], hin.at[k], s_h.at[k], hsem.at[k], {"pipe": sec + 1})
-
+    def publish(k):
         m, half = k // 2, lax.rem(k, 2)
         mine = pl.ds(pl.multiple_of(me * 128, 128), 128)
         for i in range(4):
@@ -447,27 +430,93 @@
             def _():
                 send(block, place_at, s_out.at[k, i], osem, {"expert": owner})
 
-    def turn(k, carry):
-        @pl.when((k < CHUNKS))
-        def _():
-            gather_start(k)
-            prepare(k)
-            gather_relay(k)
-
-        @pl.when((k >= 1))
-        def _():
-            home(k - 1)
-
-        @pl.when((k < CHUNKS))
-        def _():
-            feed_forward(k)
-            sum_start(k)
-            sum_relay(k)
-            sum_end(k)
-
-        return carry
-
-    lax.fori_loop(0, CHUNKS + 1, turn, 0)
+    def home(k):
+        @pl.when(sec > 0)
+        def _():
+            wait_bytes(hin.at[k], hsem.at[k])
+
+        wait_bytes(ret.at[k], retsem.at[k])
+        back = ret[k].reshape(640, 128)
+        update = jnp.dot(comb[k, 0], back, preferred_element_type=F32)
+        update = update + jnp.dot(comb[k, 1], back, preferred_element_type=F32)
+        fresh = (hin[k].astype(F32) + update).astype(BF)
+
+        @pl.when(sec < last)
+        def _():
+            place_rows(place[k], fresh, dout, k)
+            for e in far_first(1 + 2 * lax.rem(sec, 2)) + [chip * 2, chip * 2 + 1]:
+                send(
+                    dout.at[k, e], xs.at[k, 0, my_piece], s_disp.at[k], dsem.at[k, my_piece],
+                    {"pipe": sec + 1, "expert": e},
+                )
+
+        hnew[k] = fresh
+
+        @pl.when(sec < last)
+        def _():
+            send(hnew.at[k], hin.at[k], s_h.at[k], hsem.at[k], {"pipe": sec + 1})
+
+        @pl.when(sec == last)
+        def _():
+            publish(k)
+
+    @pl.when(sec == 0)
+    def _():
+        def turn(k, carry):
+            @pl.when((k < CHUNKS))
+            def _():
+                gather_start(k)
+                prepare(k)
+
+            @pl.when((k >= 1))
+            def _():
+                sum_end(k - 1)
+
+            @pl.when((k < CHUNKS))
+            def _():
+                gather_relay(k)
+                feed_forward(k)
+
+            @pl.when((k >= 1))
+            def _():
+                home(k - 1)
+
+            @pl.when((k < CHUNKS))
+            def _():
+                sum_start(k)
+                sum_relay(k)
+
+            return carry
+
+        lax.fori_loop(0, CHUNKS + 1, turn, 0)
+
+    @pl.when(sec > 0)
+    def _():
+        def turn(k, carry):
+            @pl.when((k < CHUNKS))
+            def _():
+                gather_start(k)
+                prepare(k)
+                gather_relay(k)
+
+            @pl.when((k >= 1))
+            def _():
+                home(k - 1)
+
+            @pl.when((k < CHUNKS))
+            def _():
+                feed_forward(k)
+                sum_start(k)
+                sum_relay(k)
+                sum_end(k)
+
+            return carry
+
+        lax.fori_loop(0, CHUNKS + 1, turn, 0)
+
+    @pl.when(sec < last)
+    def _():
+        lax.fori_loop(0, CHUNKS, lambda k, carry: (publish(k), carry)[1], 0)
 
     for o in range(7):
         wait_bytes(table, s_tab.at[o])

time: 283 us -> 269 us (0.951)
  Pallas kernels: 281 us -> 267 us
    pallas_call x1, Pallas kernels: 281 us -> 267 us  [local(): pl.pallas_call(relay_kernel, name='relay', out_shape=jax.ShapeDtypeStruct...]
where the time goes in v5:
time: 269 us
  Pallas kernels  267 us (99%)
    pallas_call x1, Pallas kernels, local(): pl.pallas_call(relay_kernel, name='relay', out_shape=jax.ShapeDtypeStruct...  267 us

profile of v5, /device:TPU:38, one launch (start us, length us, event | category | flops | bytes accessed | tf_op | source)
XLA Modules:
  0.0 268.6 jit_solution(6680574576218080720)
XLA Ops:
  0.0 266.9 %relay.1 = bf16[2,64,1024]{2,1,0:T(8,128)(2,1)} custom-call(bf16[2,64,4096]{2,1,0:T(8,128)(2,1)} %tokens.1, f32[1,4096]{1,0:T(1,128)} %gains.1, s32[2,2,64]{2,1,0:T(2,128)} %bitcast.15, f32[2,2,64]{2,1,0:T(2,128)} %bitcast.16, s32[2,64]{1,0:T(2,128)} %bitcast.17, bf16[4096,384]{1,0:T(8,128)(2,1)} %bitcast.11, bf16[4096,384]{1,0:T(8,128)(2,1)} %bitcast.12, ...), custom_call_target="tpu_custom_call" | custom-call | tf_op jit(solution)/shard_map/relay/pallas_call | solution.py:579
  266.9 1.7 copy.10

commit v6 on v5

--- a/solution.py
+++ b/solution.py
@@ -443,12 +443,17 @@
 
         @pl.when(sec < last)
         def _():
-            place_rows(place[k], fresh, dout, k)
-            for e in far_first(1 + 2 * lax.rem(sec, 2)) + [chip * 2, chip * 2 + 1]:
-                send(
-                    dout.at[k, e], xs.at[k, 0, my_piece], s_disp.at[k], dsem.at[k, my_piece],
-                    {"pipe": sec + 1, "expert": e},
-                )
+            side = 1 + 2 * lax.rem(sec, 2)
+            for o in (2, side, 4 - side, 0):
+                base = lax.rem(chip + o, 4) * 2
+                rows = pl.ds(pl.multiple_of(base * 80, 160), 160)
+                moved = jnp.dot(place[k, rows], fresh, preferred_element_type=F32).astype(BF)
+                for c in range(2):
+                    dout[k, base + c] = moved[c * 80 : (c + 1) * 80]
+                    send(
+                        dout.at[k, base + c], xs.at[k, 0, my_piece], s_disp.at[k], dsem.at[k, my_piece],
+                        {"pipe": sec + 1, "expert": base + c},
+                    )
 
         hnew[k] = fresh
 

time: 269 us -> 272 us (1.011)
  Pallas kernels: 267 us -> 270 us
    pallas_call x1, Pallas kernels: 267 us -> 270 us  [local(): pl.pallas_call(relay_kernel, name='relay', out_shape=jax.ShapeDtypeStruct...]
where the time goes in v6:
time: 272 us
  Pallas kernels  270 us (99%)
    pallas_call x1, Pallas kernels, local(): pl.pallas_call(relay_kernel, name='relay', out_shape=jax.ShapeDtypeStruct...  270 us

profile of v6, /device:TPU:38, one launch (start us, length us, event | category | flops | bytes accessed | tf_op | source)
XLA Modules:
  0.0 271.8 jit_solution(2469840681099345852)
XLA Ops:
  0.0 270.1 %relay.1 = bf16[2,64,1024]{2,1,0:T(8,128)(2,1)} custom-call(bf16[2,64,4096]{2,1,0:T(8,128)(2,1)} %tokens.1, f32[1,4096]{1,0:T(1,128)} %gains.1, s32[2,2,64]{2,1,0:T(2,128)} %bitcast.15, f32[2,2,64]{2,1,0:T(2,128)} %bitcast.16, s32[2,64]{1,0:T(2,128)} %bitcast.17, bf16[4096,384]{1,0:T(8,128)(2,1)} %bitcast.11, bf16[4096,384]{1,0:T(8,128)(2,1)} %bitcast.12, ...), custom_call_target="tpu_custom_call" | custom-call | tf_op jit(solution)/shard_map/relay/pallas_call | solution.py:584
  270.1 1.7 copy.10

commit v7 on v5

--- a/solution.py
+++ b/solution.py
@@ -317,9 +317,9 @@
 
     def spread_start(k):
         ssem = s_rs.at[k]
-        send(hid.at[k, 0], hid.at[k, 3], ssem, rssem.at[k, 2], {"tensor": far})
         send(hid.at[k, 0], hid.at[k, 1], ssem, rssem.at[k, 0], to_up)
         send(hid.at[k, 0], hid.at[k, 2], ssem, rssem.at[k, 1], to_dn)
+        send(hid.at[k, 0], hid.at[k, 3], ssem, rssem.at[k, 2], {"tensor": far})
         total[...] = jnp.dot(hid[k, 0], wd[rank], preferred_element_type=F32)
 
     def spread_end(k):

time: 269 us -> 271 us (level)
  no operation moved by 1% of the time
where the time goes in v7:
time: 271 us
  Pallas kernels  269 us (99%)
    pallas_call x1, Pallas kernels, local(): pl.pallas_call(relay_kernel, name='relay', out_shape=jax.ShapeDtypeStruct...  269 us

profile of v7, /device:TPU:38, one launch (start us, length us, event | category | flops | bytes accessed | tf_op | source)
XLA Modules:
  0.0 271.1 jit_solution(13047300810491973794)
XLA Ops:
  0.0 269.4 %relay.1 = bf16[2,64,1024]{2,1,0:T(8,128)(2,1)} custom-call(bf16[2,64,4096]{2,1,0:T(8,128)(2,1)} %tokens.1, f32[1,4096]{1,0:T(1,128)} %gains.1, s32[2,2,64]{2,1,0:T(2,128)} %bitcast.15, f32[2,2,64]{2,1,0:T(2,128)} %bitcast.16, s32[2,64]{1,0:T(2,128)} %bitcast.17, bf16[4096,384]{1,0:T(8,128)(2,1)} %bitcast.11, bf16[4096,384]{1,0:T(8,128)(2,1)} %bitcast.12, ...), custom_call_target="tpu_custom_call" | custom-call | tf_op jit(solution)/shard_map/relay/pallas_call | solution.py:579
  269.4 1.7 copy.10
